TPU v7x, 128 devices: a whole 4x4x4 slice. The times are simulated.
128 devices in a mesh: gx: 8 (over x, z_hi), gy: 4 (over y), gz: 4 (over z_lo, core).
Axes of the slice: x: 4, y: 4, z: 4 (z_hi: 2, z_lo: 2; z = z_hi * 2 + z_lo), core: 2. Of those that a mesh axis runs over, the one named last changes fastest.
Arguments:
- point_xyz: float32 [6144, 3, 128], P(('gx', 'gy', 'gz')), may hold values from 0 to 64, as said below
- point_weight: float32 [6144, 128], P(('gx', 'gy', 'gz')), may hold values from 0.25 to 2
- block_cell: int32 [6144], P(('gx', 'gy', 'gz')), may hold values from 0 to 8191, as said below
- block_count: int32 [6144], P(('gx', 'gy', 'gz')), may hold values from 1 to 128, as said below
- gauss_mean: float32 [8, 16, 64, 3, 32], P('gx', 'gy', 'gz'), may hold values from 0 to 64, as said below
- gauss_opacity: float32 [8, 16, 64, 32], P('gx', 'gy', 'gz'), may hold values from 0.05 to 1
- gauss_count: int32 [8, 16, 64], P('gx', 'gy', 'gz'), may hold values from 8 to 32, as said below
Outputs:
- point_out: float32 [6144, 4, 128], P(('gx', 'gy', 'gz'))
- gauss_grad: float32 [8, 16, 64, 4, 32], P('gx', 'gy', 'gz')
Inputs may be any that keep to these rules, and one draw needn't show every extreme that they name: `block_cell`: no two blocks name the same cell. Of the blocks that one device holds, at most 2 lie in the cells of any one brick (a brick is the 1 x 4 x 16 cells of one device of the grid). `block_count`: the valid points of a block are its first ones. `gauss_count`: the used slots of a cell are its first ones. `point_xyz`: every point lies in the cell of its block: each coordinate minus the cell's index lies in [0, 1]. `gauss_mean`: every centre, used or not, lies in its own cell: each coordinate minus the cell's index lies in [0, 1].
All inputs are finite; a program needn't handle non-finite values.
Results may differ from a plain program's by a relative error of at most 0.0003.
Values sent between devices are 32-bit elements; how exact they have to be, the bound alone decides.
A program may use at most 64 MiB of HBM per device.

v0:
```python
import math

import jax
import jax.numpy as jnp
from jax import lax
from jax.sharding import PartitionSpec as P

MOST = 2


kernel_width = 0.05
cutoff_sq = 0.5
floor_term = math.exp(-10.0)


def with_halo(cells, sides, width):
    for axis, dim in sides:
        count = lax.axis_size(axis)
        ends = count - 1
        head = lax.slice_in_dim(cells, 0, width, axis=dim)
        tail = lax.slice_in_dim(cells, cells.shape[dim] - width, cells.shape[dim], axis=dim)
        cells = jnp.concatenate(
            [
                lax.ppermute(tail, axis, [(i, (i + 1) % count) for i in range(ends)]),
                cells,
                lax.ppermute(head, axis, [((i + 1) % count, i) for i in range(ends)]),
            ],
            axis=dim,
        )
    return cells


def window(values, step_x, step_y, step_z, extent):
    anchor = jnp.zeros((), jnp.int32)
    corner = (step_x, step_y, step_z) + (anchor,) * (values.ndim - 3)
    return lax.dynamic_slice(values, corner, tuple(extent) + values.shape[3:])


def put_window(values, update, step_x, step_y, step_z):
    anchor = jnp.zeros((), jnp.int32)
    corner = (step_x, step_y, step_z) + (anchor,) * (values.ndim - 3)
    return lax.dynamic_update_slice(values, update, corner)


def pair_block(own_items, own_inv, far_items, far_inv, second):
    delta_x = own_items[..., 0, :, None] - far_items[..., 0, None, :]
    delta_y = own_items[..., 1, :, None] - far_items[..., 1, None, :]
    delta_z = own_items[..., 2, :, None] - far_items[..., 2, None, :]
    distance = delta_x * delta_x + delta_y * delta_y + delta_z * delta_z
    falloff = jnp.exp(-distance / cutoff_sq)
    kernel = jnp.exp((falloff - 1.0) * (cutoff_sq / kernel_width))
    own_wt = own_items[..., 3, :, None]
    far_wt = far_items[..., 3, None, :]
    if not second:
        own_sum = jnp.sum(kernel * far_wt, axis=-1)
        far_sum = jnp.sum(kernel * own_wt, axis=-2)
        return (own_sum, far_sum)
    coupling = (
        2.0 * own_wt * far_wt * kernel * falloff * (own_inv[..., :, None] + far_inv[..., None, :])
    )
    own_grad = jnp.stack(
        [
            jnp.sum(coupling * delta_x, axis=-1),
            jnp.sum(coupling * delta_y, axis=-1),
            jnp.sum(coupling * delta_z, axis=-1),
        ],
        axis=-2,
    )
    far_out = None
    far_grad = -jnp.stack(
        [
            jnp.sum(coupling * delta_x, axis=-2),
            jnp.sum(coupling * delta_y, axis=-2),
            jnp.sum(coupling * delta_z, axis=-2),
        ],
        axis=-2,
    )
    far_density = jnp.sum(kernel * own_wt * own_inv[..., :, None], axis=-2)
    far_out = jnp.concatenate([far_grad, far_density[..., None, :]], axis=-2)
    return (own_grad, far_out)


def sweep_pairs(own_items, own_inv, far_grid, far_inv, second):
    extent = own_items.shape[:3]
    own_len = own_items.shape[-1]
    far_len = far_grid.shape[-1]
    if second:
        own_acc = jnp.zeros(extent + (3, own_len), jnp.float32)
        far_acc = jnp.zeros(far_grid.shape[:3] + (4, far_len), jnp.float32)
    else:
        own_acc = jnp.zeros(extent + (own_len,), jnp.float32)
        far_acc = jnp.zeros(far_grid.shape[:3] + (far_len,), jnp.float32)

    def one_offset(offset, state_pair):
        own_total, far_total = state_pair
        step_x = (offset // 9).astype(jnp.int32)
        step_y = (offset // 3 % 3).astype(jnp.int32)
        step_z = (offset % 3).astype(jnp.int32)
        far_items = window(far_grid, step_x, step_y, step_z, extent)
        far_part_inv = window(far_inv, step_x, step_y, step_z, extent) if second else None
        own_part, far_part = pair_block(own_items, own_inv, far_items, far_part_inv, second)
        own_total = own_total + own_part
        region = window(far_total, step_x, step_y, step_z, extent) + far_part
        far_total = put_window(far_total, region, step_x, step_y, step_z)
        return (own_total, far_total)

    return lax.fori_loop(0, 27, one_offset, (own_acc, far_acc))


def fold_rim(values):
    for dim_index in range(3):
        inner_len = values.shape[dim_index] - 4
        middle = lax.slice_in_dim(values, 2, inner_len + 2, axis=dim_index)
        lower_rim = lax.slice_in_dim(values, 0, 1, axis=dim_index)
        upper_rim = lax.slice_in_dim(values, inner_len + 3, inner_len + 4, axis=dim_index)
        widths_low = [(0, 0)] * values.ndim
        widths_low[dim_index] = (0, inner_len - 1)
        widths_high = [(0, 0)] * values.ndim
        widths_high[dim_index] = (inner_len - 1, 0)
        values = middle + jnp.pad(lower_rim, widths_low) + jnp.pad(upper_rim, widths_high)
    return values


def on_device(
    point_xyz, point_weight, block_cell, block_count, gauss_mean, gauss_opacity, gauss_count
):
    points_len = point_xyz.shape[2]
    span_x, span_y, span_z, unused_dim, gauss_slots = gauss_mean.shape
    size_x = lax.axis_size("gx")
    size_y = lax.axis_size("gy")
    size_z = lax.axis_size("gz")
    bricks = size_x * size_y * size_z
    cell_total = span_x * span_y * span_z
    depth_y = span_y * size_y
    depth_z = span_z * size_z
    along_x = block_cell // (depth_y * depth_z)
    along_y = block_cell // depth_z % depth_y
    along_z = block_cell % depth_z
    target = (along_x // span_x * size_y + along_y // span_y) * size_z + along_z // span_z
    local_cell = (along_x % span_x * span_y + along_y % span_y) * span_z + along_z % span_z
    chosen = (target[:, None] == jnp.arange(bricks, dtype=jnp.int32)[None, :]).astype(jnp.int32)
    before = jnp.sum((jnp.cumsum(chosen, axis=0) - chosen) * chosen, axis=1)
    send_slot = target * MOST + before
    is_valid = jnp.arange(points_len, dtype=jnp.int32)[None, :] < block_count[:, None]
    weights = jnp.where(is_valid, point_weight, 0.0)
    payload = jnp.concatenate([point_xyz, weights[:, None, :]], axis=1)
    outgoing = jnp.zeros((bricks * MOST, 4, points_len), jnp.float32).at[send_slot].set(payload)
    labels = jnp.full((bricks * MOST,), -1, jnp.int32).at[send_slot].set(local_cell)
    incoming, arrived = (
        lax.all_to_all(outgoing, ("gx", "gy", "gz"), split_axis=0, concat_axis=0, tiled=True),
        lax.all_to_all(labels, ("gx", "gy", "gz"), split_axis=0, concat_axis=0, tiled=True),
    )
    placed = jnp.where(arrived >= 0, arrived, cell_total)
    points = (
        jnp.zeros((cell_total, 4, points_len), jnp.float32).at[placed].set(incoming, mode="drop")
    )
    points = points.reshape(span_x, span_y, span_z, 4, points_len)
    present = jnp.arange(gauss_slots, dtype=jnp.int32) < gauss_count[..., None]
    gaussians = jnp.concatenate(
        [gauss_mean, jnp.where(present, gauss_opacity, 0.0)[..., None, :]], axis=3
    )
    far_gauss = with_halo(gaussians, (("gx", 0), ("gy", 1), ("gz", 2)), 1)
    density_p, density_far = sweep_pairs(points, None, far_gauss, None, False)
    density_g = fold_rim(with_halo(density_far, (("gx", 0), ("gy", 1), ("gz", 2)), 1))
    total_p = floor_term + density_p
    total_g = floor_term + density_g
    inverse_p = 1.0 / total_p
    inverse_g = 1.0 / total_g
    far_inverse = with_halo(inverse_g, (("gx", 0), ("gy", 1), ("gz", 2)), 1)
    gradient_p, gradient_far = sweep_pairs(points, inverse_p, far_gauss, far_inverse, True)
    gradient_g = fold_rim(with_halo(gradient_far, (("gx", 0), ("gy", 1), ("gz", 2)), 1))
    loss_p = jnp.where(points[..., 3, :] > 0.0, -kernel_width * jnp.log(total_p), 0.0)
    cell_result = jnp.concatenate([loss_p[..., None, :], gradient_p], axis=3).reshape(
        cell_total, 4, points_len
    )
    reply_rows = jnp.where(
        (arrived >= 0)[:, None, None], cell_result[jnp.clip(arrived, 0, cell_total - 1)], 0.0
    )
    answer = lax.all_to_all(reply_rows, ("gx", "gy", "gz"), split_axis=0, concat_axis=0, tiled=True)
    point_out = answer[send_slot]
    grad_opacity = jnp.where(
        present, -kernel_width * jnp.log(total_g) - kernel_width * gradient_g[..., 3, :], 0.0
    )
    gauss_grad = jnp.concatenate([gradient_g[..., :3, :], grad_opacity[..., None, :]], axis=3)
    return (point_out, gauss_grad)


def solution(mesh):
    return jax.shard_map(
        on_device,
        mesh=mesh,
        in_specs=(
            P(("gx", "gy", "gz"), None, None),
            P(("gx", "gy", "gz"), None),
            P(("gx", "gy", "gz")),
            P(("gx", "gy", "gz")),
            P("gx", "gy", "gz", None, None),
            P("gx", "gy", "gz", None),
            P("gx", "gy", "gz"),
        ),
        out_specs=(P(("gx", "gy", "gz"), None, None), P("gx", "gy", "gz", None, None)),
        check_vma=False,
    )
```

profile of v0, /device:TPU:1, one launch (start us, length us, event | category | flops | bytes accessed | tf_op | source)
XLA Modules:
  0.0 340.2 jit_solution(11961913342789232397)
XLA Ops:
  3.7 7.0 %collective-permute-start = (f32[1,4,16,4,32]{4,2,1,3,0:T(8,128)S(1)}, f32[1,4,16,4,32]{4,2,1,3,0:T(8,128)S(1)}, u32[]{:S(2)}, u32[]{:S(2)}) collective-permute-start(f32[1,4,16,4,32]{4,2,1,3,0:T(8,128)S(1)} %pad_maximum_fusion.6), channel_id=1, source_target_pairs={{0,16},{16,32},{32,48},{48,64},{64,80},{80,96},{96,112},{1,17},{17... | collective-permute-start | bytes 98312 | tf_op jit(solution)/shard_map/ppermute | solution.py:24
  13.8 11.5 %all-to-all-start = ((s32[128,2,1]{1,2,0:T(1,128)}), s32[128,2,1]{1,2,0:T(1,128)S(1)}, u32[]{:S(2)}, u32[]{:S(2)}) async-start(s32[128,2,1]{1,2,0:T(1,128)} %bitcast), calls=%async_computation | async-start | bytes 131072 | tf_op jit(solution)/shard_map/all_to_all | solution.py:151
  27.0 3.3 collective-permute-start.2
  33.4 5.0 %scatter_fusion = f32[256,4,128]{2,1,0:T(4,128)} fusion(f32[256,4,128]{2,1,0:T(4,128)} %broadcast_in_dim.90, s32[48]{0:T(128)S(1)} %compare_select_fusion.3, f32[48,4,128]{2,1,0:T(4,128)S(1)} %copy.41), kind=kCustom, calls=%fused_computation.3 | custom fusion | bytes 295104 | tf_op jit(solution)/shard_map/scatter | solution.py:147
  38.4 11.0 %all-to-all-start.1 = ((f32[256,4,128]{2,1,0:T(4,128)}), f32[256,4,128]{2,1,0:T(4,128)S(1)}, u32[]{:S(2)}, u32[]{:S(2)}) async-start(f32[256,4,128]{2,1,0:T(4,128)} %scatter_fusion), calls=%async_computation.1 | async-start | bytes 1048576 | tf_op jit(solution)/shard_map/all_to_all | solution.py:150
  51.0 3.7 %collective-permute-start.4 = (f32[3,6,1,4,32]{4,2,1,3,0:T(1,128)S(1)}, f32[3,6,1,4,32]{4,2,1,3,0:T(1,128)S(1)}, u32[]{:S(2)}, u32[]{:S(2)}) collective-permute-start(f32[3,6,1,4,32]{4,2,1,3,0:T(1,128)S(1)} %get-tuple-element.494), channel_id=1, source_target_pairs={{0,1},{1,2},{2,3},{4,5},{5,6},{6,7},{8,9},{9,10},{10,11},{12,13},{... | collective-permute-start | bytes 27656 | tf_op jit(solution)/shard_map/ppermute | solution.py:24
  56.6 3.8 %collective-permute-done.5 = f32[3,6,1,4,32]{4,2,1,3,0:T(1,128)S(1)} collective-permute-done((f32[3,6,1,4,32]{4,2,1,3,0:T(1,128)S(1)}, f32[3,6,1,4,32]{4,2,1,3,0:T(1,128)S(1)}, u32[]{:S(2)}, u32[]{:S(2)}) %collective-permute-start.5) | collective-permute-done | bytes 9248 | tf_op jit(solution)/shard_map/ppermute | solution.py:26
  63.4 7.6 %scatter_fusion.1 = f32[64,4,128]{2,1,0:T(4,128)S(1)} fusion(f32[64,4,128]{2,1,0:T(4,128)S(1)} %broadcast_in_dim.88, s32[256]{0:T(256)S(1)} %bitcast.121, f32[256,4,128]{2,1,0:T(4,128)S(1)} %all-to-all-done.1), kind=kCustom, calls=%fused_computation.4 | custom fusion | bytes 1573888 | tf_op jit(solution)/shard_map/scatter | solution.py:155
  71.1 60.9 %while.38 = (s32[]{:T(128)}, f32[1,4,16,128]{3,2,1,0:T(8,128)S(1)}, f32[3,6,18,32]{3,2,1,0:T(8,128)S(1)}, f32[1,4,16,4,128]{4,2,1,3,0:T(8,128)S(1)}, f32[3,6,18,...) while((s32[]{:T(128)}, f32[1,4,16,128]{3,2,1,0:T(8,128)S(1)}, ...), condition=%wide.region_8.9_spmd.clone, body=%wide.region_5.8_spmd.clone.sunk | while | flops 4202535 | bytes 672315 | solution.py:107
  135.8 5.2 %collective-permute-done.7 = f32[1,6,18,32]{3,2,1,0:T(8,128)S(1)} collective-permute-done((f32[1,6,18,32]{3,2,1,0:T(8,128)S(1)}, f32[1,6,18,32]{3,2,1,0:T(8,128)S(1)}, u32[]{:S(2)}, u32[]{:S(2)}) %collective-permute-start.7) | collective-permute-done | bytes 13856 | tf_op jit(solution)/shard_map/ppermute | solution.py:26
  145.1 4.0 %collective-permute-done.9 = f32[5,1,18,32]{3,2,1,0:T(8,128)S(1)} collective-permute-done((f32[5,1,18,32]{3,2,1,0:T(8,128)S(1)}, f32[5,1,18,32]{3,2,1,0:T(8,128)S(1)}, u32[]{:S(2)}, u32[]{:S(2)}) %collective-permute-start.9) | collective-permute-done | bytes 11552 | tf_op jit(solution)/shard_map/ppermute | solution.py:26
  149.1 4.4 %collective-permute-start.10 = (f32[5,8,1,32]{3,2,1,0:T(1,128)S(1)}, f32[5,8,1,32]{3,2,1,0:T(1,128)S(1)}, u32[]{:S(2)}, u32[]{:S(2)}) collective-permute-start(f32[5,8,1,32]{3,2,1,0:T(1,128)S(1)} %get-tuple-element.496), channel_id=1, source_target_pairs={{0,1},{1,2},{2,3},{4,5},{5,6},{6,7},{8,9},{9,10},{10,11},{12,13},{... | collective-permute-start | bytes 15368 | tf_op jit(solution)/shard_map/ppermute | solution.py:24
  160.3 7.0 %collective-permute-start.12 = (f32[1,4,16,32]{3,2,1,0:T(8,128)S(1)}, f32[1,4,16,32]{3,2,1,0:T(8,128)S(1)}, u32[]{:S(2)}, u32[]{:S(2)}) collective-permute-start(f32[1,4,16,32]{3,2,1,0:T(8,128)S(1)} %broadcast_divide_fusion), channel_id=1, source_target_pairs={{0,16},{16,32},{32,48},{48,64},{64,80},{80,96},{96,112},{1,17},{17... | collective-permute-start | bytes 24584 | tf_op jit(solution)/shard_map/ppermute | solution.py:24
  171.4 3.0 collective-permute-done.15
  174.5 3.9 %collective-permute-start.16 = (f32[3,6,1,32]{3,2,1,0:T(1,128)S(1)}, f32[3,6,1,32]{3,2,1,0:T(1,128)S(1)}, u32[]{:S(2)}, u32[]{:S(2)}) collective-permute-start(f32[3,6,1,32]{3,2,1,0:T(1,128)S(1)} %get-tuple-element.504), channel_id=1, source_target_pairs={{0,1},{1,2},{2,3},{4,5},{5,6},{6,7},{8,9},{9,10},{10,11},{12,13},{... | collective-permute-start | bytes 6920 | tf_op jit(solution)/shard_map/ppermute | solution.py:24
  183.5 96.5 %while.39 = (s32[]{:T(128)}, f32[1,4,16,3,128]{4,2,1,3,0:T(8,128)S(1)}, f32[3,6,18,4,32]{4,2,1,3,0:T(8,128)S(1)}, f32[1,4,16,4,128]{4,2,1,3,0:T(8,128)S(1)}, f32...) while((s32[]{:T(128)}, ...), condition=%wide.region_17.18_spmd.clone, body=%wide.region_9.17_spmd.clone.sunk | while | flops 7710759 | bytes 1286743 | solution.py:107
  183.7 3.0 fusion.41
  190.8 3.0 fusion.41
  194.4 3.0 fusion.41
  201.5 3.0 fusion.41
  205.1 3.0 fusion.41
  212.3 3.0 fusion.41
  215.8 3.0 fusion.41
  223.0 3.0 fusion.41
  226.5 3.0 fusion.41
  280.0 6.4 %collective-permute-start.18 = (f32[1,6,18,4,32]{4,2,1,3,0:T(8,128)S(1)}, f32[1,6,18,4,32]{4,2,1,3,0:T(8,128)S(1)}, u32[]{:S(2)}, u32[]{:S(2)}) collective-permute-start(f32[1,6,18,4,32]{4,2,1,3,0:T(8,128)S(1)} %get-tuple-element.493), channel_id=1, source_target_pairs={{0,16},{16,32},{32,48},{48,64},{64,80},{80,96},{96,112},{1,17},{17... | collective-permute-start | bytes 165896 | tf_op jit(solution)/shard_map/ppermute | solution.py:24
  288.0 3.8 %collective-permute-done.18 = f32[1,6,18,4,32]{4,2,1,3,0:T(8,128)S(1)} collective-permute-done((f32[1,6,18,4,32]{4,2,1,3,0:T(8,128)S(1)}, f32[1,6,18,4,32]{4,2,1,3,0:T(8,128)S(1)}, u32[]{:S(2)}, u32[]{:S(2)}) %collective-permute-start.18) | collective-permute-done | bytes 55328 | tf_op jit(solution)/shard_map/ppermute | solution.py:24
  291.9 6.4 %collective-permute-done.19 = f32[1,6,18,4,32]{4,2,1,3,0:T(8,128)S(1)} collective-permute-done((f32[1,6,18,4,32]{4,2,1,3,0:T(8,128)S(1)}, f32[1,6,18,4,32]{4,2,1,3,0:T(8,128)S(1)}, u32[]{:S(2)}, u32[]{:S(2)}) %collective-permute-start.19) | collective-permute-done | bytes 55328 | tf_op jit(solution)/shard_map/ppermute | solution.py:26
  303.5 3.1 collective-permute-done.20
  306.6 4.4 %collective-permute-done.21 = f32[5,1,18,4,32]{4,2,1,3,0:T(8,128)S(1)} collective-permute-done((f32[5,1,18,4,32]{4,2,1,3,0:T(8,128)S(1)}, f32[5,1,18,4,32]{4,2,1,3,0:T(8,128)S(1)}, u32[]{:S(2)}, u32[]{:S(2)}) %collective-permute-start.21) | collective-permute-done | bytes 46112 | tf_op jit(solution)/shard_map/ppermute | solution.py:26
  316.6 8.3 %all-to-all-start.2 = ((f32[256,4,128]{2,1,0:T(4,128)}), f32[256,4,128]{2,1,0:T(4,128)S(1)}, u32[]{:S(2)}, u32[]{:S(2)}) async-start(f32[256,4,128]{2,1,0:T(4,128)} %broadcast_select_fusion), calls=%async_computation.2 | async-start | bytes 1048576 | tf_op jit(solution)/shard_map/all_to_all | solution.py:179
  326.5 12.4 %all-to-all-done.2 = f32[256,4,128]{2,1,0:T(4,128)S(1)} async-done(((f32[256,4,128]{2,1,0:T(4,128)}), f32[256,4,128]{2,1,0:T(4,128)S(1)}, u32[]{:S(2)}, u32[]{:S(2)}) %all-to-all-start.2) | async-done | bytes 524320 | tf_op jit(solution)/shard_map/all_to_all | solution.py:179
  (505 shorter events, 178.2 us)
Async XLA Ops:
  2.4 23.8 %collective-permute-start.1 = (f32[1,4,16,4,32]{4,2,1,3,0:T(8,128)S(1)}, f32[1,4,16,4,32]{4,2,1,3,0:T(8,128)S(1)}, u32[]{:S(2)}, u32[]{:S(2)}) collective-permute-start(f32[1,4,16,4,32]{4,2,1,3,0:T(8,128)S(1)} %pad_maximum_fusion.6), channel_id=1, source_target_pairs={{16,0},{32,16},{48,32},{64,48},{80,64},{96,80},{112,96},{17,1},{33... | collective-permute-start | bytes 98312 | tf_op jit(solution)/shard_map/ppermute | solution.py:26
  3.7 22.5 %collective-permute-start = (f32[1,4,16,4,32]{4,2,1,3,0:T(8,128)S(1)}, f32[1,4,16,4,32]{4,2,1,3,0:T(8,128)S(1)}, u32[]{:S(2)}, u32[]{:S(2)}) collective-permute-start(f32[1,4,16,4,32]{4,2,1,3,0:T(8,128)S(1)} %pad_maximum_fusion.6), channel_id=1, source_target_pairs={{0,16},{16,32},{32,48},{48,64},{64,80},{80,96},{96,112},{1,17},{17... | collective-permute-start | bytes 98312 | tf_op jit(solution)/shard_map/ppermute | solution.py:24
  13.8 24.6 %all-to-all-start = ((s32[128,2,1]{1,2,0:T(1,128)}), s32[128,2,1]{1,2,0:T(1,128)S(1)}, u32[]{:S(2)}, u32[]{:S(2)}) async-start(s32[128,2,1]{1,2,0:T(1,128)} %bitcast), calls=%async_computation | async-start | bytes 131072 | tf_op jit(solution)/shard_map/all_to_all | solution.py:151
  26.1 24.8 %copy-start = (f32[1,4,16,3,32]{4,2,3,1,0:T(8,128)S(1)}, f32[1,4,16,3,32]{4,2,3,1,0:T(8,128)}, u32[]{:S(2)}) copy-start(f32[1,4,16,3,32]{4,2,3,1,0:T(8,128)} %param.15) | copy-start | bytes 73732
  27.0 23.9 %collective-permute-start.2 = (f32[3,1,16,4,32]{4,2,1,3,0:T(8,128)S(1)}, f32[3,1,16,4,32]{4,2,1,3,0:T(8,128)S(1)}, u32[]{:S(2)}, u32[]{:S(2)}) collective-permute-start(f32[3,1,16,4,32]{4,2,1,3,0:T(8,128)S(1)} %get-tuple-element.498), channel_id=1, source_target_pairs={{0,4},{4,8},{8,12},{1,5},{5,9},{9,13},{2,6},{6,10},{10,14},{3,7},{... | collective-permute-start | bytes 73736 | tf_op jit(solution)/shard_map/ppermute | solution.py:24
  30.3 20.6 %collective-permute-start.3 = (f32[3,1,16,4,32]{4,2,1,3,0:T(8,128)S(1)}, f32[3,1,16,4,32]{4,2,1,3,0:T(8,128)S(1)}, u32[]{:S(2)}, u32[]{:S(2)}) collective-permute-start(f32[3,1,16,4,32]{4,2,1,3,0:T(8,128)S(1)} %get-tuple-element.499), channel_id=1, source_target_pairs={{4,0},{8,4},{12,8},{5,1},{9,5},{13,9},{6,2},{10,6},{14,10},{7,3},{... | collective-permute-start | bytes 73736 | tf_op jit(solution)/shard_map/ppermute | solution.py:26
  38.4 25.0 %all-to-all-start.1 = ((f32[256,4,128]{2,1,0:T(4,128)}), f32[256,4,128]{2,1,0:T(4,128)S(1)}, u32[]{:S(2)}, u32[]{:S(2)}) async-start(f32[256,4,128]{2,1,0:T(4,128)} %scatter_fusion), calls=%async_computation.1 | async-start | bytes 1048576 | tf_op jit(solution)/shard_map/all_to_all | solution.py:150
  51.0 5.6 %collective-permute-start.4 = (f32[3,6,1,4,32]{4,2,1,3,0:T(1,128)S(1)}, f32[3,6,1,4,32]{4,2,1,3,0:T(1,128)S(1)}, u32[]{:S(2)}, u32[]{:S(2)}) collective-permute-start(f32[3,6,1,4,32]{4,2,1,3,0:T(1,128)S(1)} %get-tuple-element.494), channel_id=1, source_target_pairs={{0,1},{1,2},{2,3},{4,5},{5,6},{6,7},{8,9},{9,10},{10,11},{12,13},{... | collective-permute-start | bytes 27656 | tf_op jit(solution)/shard_map/ppermute | solution.py:24
  54.7 5.7 %collective-permute-start.5 = (f32[3,6,1,4,32]{4,2,1,3,0:T(1,128)S(1)}, f32[3,6,1,4,32]{4,2,1,3,0:T(1,128)S(1)}, u32[]{:S(2)}, u32[]{:S(2)}) collective-permute-start(f32[3,6,1,4,32]{4,2,1,3,0:T(1,128)S(1)} %get-tuple-element.495), channel_id=1, source_target_pairs={{1,0},{2,1},{3,2},{5,4},{6,5},{7,6},{9,8},{10,9},{11,10},{13,12},{... | collective-permute-start | bytes 27656 | tf_op jit(solution)/shard_map/ppermute | solution.py:26
  132.1 26.7 %copy-start.3 = (pred[4]{0:T(512)(128)(4,1)S(1)}, pred[4]{0:T(512)(128)(4,1)}, u32[]{:S(2)}) copy-start(pred[4]{0:T(512)(128)(4,1)} %constant.400.clone.1) | copy-start | bytes 16
  132.1 26.8 %copy-start.2 = (pred[16]{0:T(512)(128)(4,1)S(1)}, pred[16]{0:T(512)(128)(4,1)}, u32[]{:S(2)}) copy-start(pred[16]{0:T(512)(128)(4,1)} %constant.401.clone.1) | copy-start | bytes 52
  132.1 3.7 %collective-permute-start.6 = (f32[1,6,18,32]{3,2,1,0:T(8,128)S(1)}, f32[1,6,18,32]{3,2,1,0:T(8,128)S(1)}, u32[]{:S(2)}, u32[]{:S(2)}) collective-permute-start(f32[1,6,18,32]{3,2,1,0:T(8,128)S(1)} %get-tuple-element.503), channel_id=1, source_target_pairs={{0,16},{16,32},{32,48},{48,64},{64,80},{80,96},{96,112},{1,17},{17... | collective-permute-start | bytes 41480 | tf_op jit(solution)/shard_map/ppermute | solution.py:24
  134.4 6.6 %collective-permute-start.7 = (f32[1,6,18,32]{3,2,1,0:T(8,128)S(1)}, f32[1,6,18,32]{3,2,1,0:T(8,128)S(1)}, u32[]{:S(2)}, u32[]{:S(2)}) collective-permute-start(f32[1,6,18,32]{3,2,1,0:T(8,128)S(1)} %get-tuple-element.502), channel_id=1, source_target_pairs={{16,0},{32,16},{48,32},{64,48},{80,64},{96,80},{112,96},{17,1},{33... | collective-permute-start | bytes 41480 | tf_op jit(solution)/shard_map/ppermute | solution.py:26
  141.0 4.0 %collective-permute-start.8 = (f32[5,1,18,32]{3,2,1,0:T(8,128)S(1)}, f32[5,1,18,32]{3,2,1,0:T(8,128)S(1)}, u32[]{:S(2)}, u32[]{:S(2)}) collective-permute-start(f32[5,1,18,32]{3,2,1,0:T(8,128)S(1)} %get-tuple-element.500), channel_id=1, source_target_pairs={{0,4},{4,8},{8,12},{1,5},{5,9},{9,13},{2,6},{6,10},{10,14},{3,7},{... | collective-permute-start | bytes 34568 | tf_op jit(solution)/shard_map/ppermute | solution.py:24
  143.8 5.3 %collective-permute-start.9 = (f32[5,1,18,32]{3,2,1,0:T(8,128)S(1)}, f32[5,1,18,32]{3,2,1,0:T(8,128)S(1)}, u32[]{:S(2)}, u32[]{:S(2)}) collective-permute-start(f32[5,1,18,32]{3,2,1,0:T(8,128)S(1)} %get-tuple-element.501), channel_id=1, source_target_pairs={{4,0},{8,4},{12,8},{5,1},{9,5},{13,9},{6,2},{10,6},{14,10},{7,3},{... | collective-permute-start | bytes 34568 | tf_op jit(solution)/shard_map/ppermute | solution.py:26
  149.1 6.7 %collective-permute-start.10 = (f32[5,8,1,32]{3,2,1,0:T(1,128)S(1)}, f32[5,8,1,32]{3,2,1,0:T(1,128)S(1)}, u32[]{:S(2)}, u32[]{:S(2)}) collective-permute-start(f32[5,8,1,32]{3,2,1,0:T(1,128)S(1)} %get-tuple-element.496), channel_id=1, source_target_pairs={{0,1},{1,2},{2,3},{4,5},{5,6},{6,7},{8,9},{9,10},{10,11},{12,13},{... | collective-permute-start | bytes 15368 | tf_op jit(solution)/shard_map/ppermute | solution.py:24
  153.6 5.1 %collective-permute-start.11 = (f32[5,8,1,32]{3,2,1,0:T(1,128)S(1)}, f32[5,8,1,32]{3,2,1,0:T(1,128)S(1)}, u32[]{:S(2)}, u32[]{:S(2)}) collective-permute-start(f32[5,8,1,32]{3,2,1,0:T(1,128)S(1)} %get-tuple-element.497), channel_id=1, source_target_pairs={{1,0},{2,1},{3,2},{5,4},{6,5},{7,6},{9,8},{10,9},{11,10},{13,12},{... | collective-permute-start | bytes 15368 | tf_op jit(solution)/shard_map/ppermute | solution.py:26
  159.0 8.3 %collective-permute-start.13 = (f32[1,4,16,32]{3,2,1,0:T(8,128)S(1)}, f32[1,4,16,32]{3,2,1,0:T(8,128)S(1)}, u32[]{:S(2)}, u32[]{:S(2)}) collective-permute-start(f32[1,4,16,32]{3,2,1,0:T(8,128)S(1)} %broadcast_divide_fusion), channel_id=1, source_target_pairs={{16,0},{32,16},{48,32},{64,48},{80,64},{96,80},{112,96},{17,1},{33... | collective-permute-start | bytes 24584 | tf_op jit(solution)/shard_map/ppermute | solution.py:26
  160.3 8.0 %collective-permute-start.12 = (f32[1,4,16,32]{3,2,1,0:T(8,128)S(1)}, f32[1,4,16,32]{3,2,1,0:T(8,128)S(1)}, u32[]{:S(2)}, u32[]{:S(2)}) collective-permute-start(f32[1,4,16,32]{3,2,1,0:T(8,128)S(1)} %broadcast_divide_fusion), channel_id=1, source_target_pairs={{0,16},{16,32},{32,48},{48,64},{64,80},{80,96},{96,112},{1,17},{17... | collective-permute-start | bytes 24584 | tf_op jit(solution)/shard_map/ppermute | solution.py:24
  168.3 3.2 collective-permute-start.14
  169.9 4.6 %collective-permute-start.15 = (f32[3,1,16,32]{3,2,1,0:T(8,128)S(1)}, f32[3,1,16,32]{3,2,1,0:T(8,128)S(1)}, u32[]{:S(2)}, u32[]{:S(2)}) collective-permute-start(f32[3,1,16,32]{3,2,1,0:T(8,128)S(1)} %get-tuple-element.507), channel_id=1, source_target_pairs={{4,0},{8,4},{12,8},{5,1},{9,5},{13,9},{6,2},{10,6},{14,10},{7,3},{... | collective-permute-start | bytes 18440 | tf_op jit(solution)/shard_map/ppermute | solution.py:26
  174.5 5.8 %collective-permute-start.16 = (f32[3,6,1,32]{3,2,1,0:T(1,128)S(1)}, f32[3,6,1,32]{3,2,1,0:T(1,128)S(1)}, u32[]{:S(2)}, u32[]{:S(2)}) collective-permute-start(f32[3,6,1,32]{3,2,1,0:T(1,128)S(1)} %get-tuple-element.504), channel_id=1, source_target_pairs={{0,1},{1,2},{2,3},{4,5},{5,6},{6,7},{8,9},{9,10},{10,11},{12,13},{... | collective-permute-start | bytes 6920 | tf_op jit(solution)/shard_map/ppermute | solution.py:24
  178.4 5.0 %collective-permute-start.17 = (f32[3,6,1,32]{3,2,1,0:T(1,128)S(1)}, f32[3,6,1,32]{3,2,1,0:T(1,128)S(1)}, u32[]{:S(2)}, u32[]{:S(2)}) collective-permute-start(f32[3,6,1,32]{3,2,1,0:T(1,128)S(1)} %get-tuple-element.505), channel_id=1, source_target_pairs={{1,0},{2,1},{3,2},{5,4},{6,5},{7,6},{9,8},{10,9},{11,10},{13,12},{... | collective-permute-start | bytes 6920 | tf_op jit(solution)/shard_map/ppermute | solution.py:26
  280.0 11.8 %collective-permute-start.18 = (f32[1,6,18,4,32]{4,2,1,3,0:T(8,128)S(1)}, f32[1,6,18,4,32]{4,2,1,3,0:T(8,128)S(1)}, u32[]{:S(2)}, u32[]{:S(2)}) collective-permute-start(f32[1,6,18,4,32]{4,2,1,3,0:T(8,128)S(1)} %get-tuple-element.493), channel_id=1, source_target_pairs={{0,16},{16,32},{32,48},{48,64},{64,80},{80,96},{96,112},{1,17},{17... | collective-permute-start | bytes 165896 | tf_op jit(solution)/shard_map/ppermute | solution.py:24
  286.7 11.6 %collective-permute-start.19 = (f32[1,6,18,4,32]{4,2,1,3,0:T(8,128)S(1)}, f32[1,6,18,4,32]{4,2,1,3,0:T(8,128)S(1)}, u32[]{:S(2)}, u32[]{:S(2)}) collective-permute-start(f32[1,6,18,4,32]{4,2,1,3,0:T(8,128)S(1)} %get-tuple-element.492), channel_id=1, source_target_pairs={{16,0},{32,16},{48,32},{64,48},{80,64},{96,80},{112,96},{17,1},{33... | collective-permute-start | bytes 165896 | tf_op jit(solution)/shard_map/ppermute | solution.py:26
  298.3 8.3 %collective-permute-start.20 = (f32[5,1,18,4,32]{4,2,1,3,0:T(8,128)S(1)}, f32[5,1,18,4,32]{4,2,1,3,0:T(8,128)S(1)}, u32[]{:S(2)}, u32[]{:S(2)}) collective-permute-start(f32[5,1,18,4,32]{4,2,1,3,0:T(8,128)S(1)} %get-tuple-element.490), channel_id=1, source_target_pairs={{0,4},{4,8},{8,12},{1,5},{5,9},{9,13},{2,6},{6,10},{10,14},{3,7},{... | collective-permute-start | bytes 138248 | tf_op jit(solution)/shard_map/ppermute | solution.py:24
  301.1 9.8 %collective-permute-start.21 = (f32[5,1,18,4,32]{4,2,1,3,0:T(8,128)S(1)}, f32[5,1,18,4,32]{4,2,1,3,0:T(8,128)S(1)}, u32[]{:S(2)}, u32[]{:S(2)}) collective-permute-start(f32[5,1,18,4,32]{4,2,1,3,0:T(8,128)S(1)} %get-tuple-element.491), channel_id=1, source_target_pairs={{4,0},{8,4},{12,8},{5,1},{9,5},{13,9},{6,2},{10,6},{14,10},{7,3},{... | collective-permute-start | bytes 138248 | tf_op jit(solution)/shard_map/ppermute | solution.py:26
  311.1 13.8 %collective-permute-start.22 = (f32[5,8,1,4,32]{4,2,1,3,0:T(1,128)S(1)}, f32[5,8,1,4,32]{4,2,1,3,0:T(1,128)S(1)}, u32[]{:S(2)}, u32[]{:S(2)}) collective-permute-start(f32[5,8,1,4,32]{4,2,1,3,0:T(1,128)S(1)} %get-tuple-element.488), channel_id=1, source_target_pairs={{0,1},{1,2},{2,3},{4,5},{5,6},{6,7},{8,9},{9,10},{10,11},{12,13},{... | collective-permute-start | bytes 61448 | tf_op jit(solution)/shard_map/ppermute | solution.py:24
  313.1 11.8 %collective-permute-start.23 = (f32[5,8,1,4,32]{4,2,1,3,0:T(1,128)S(1)}, f32[5,8,1,4,32]{4,2,1,3,0:T(1,128)S(1)}, u32[]{:S(2)}, u32[]{:S(2)}) collective-permute-start(f32[5,8,1,4,32]{4,2,1,3,0:T(1,128)S(1)} %get-tuple-element.489), channel_id=1, source_target_pairs={{1,0},{2,1},{3,2},{5,4},{6,5},{7,6},{9,8},{10,9},{11,10},{13,12},{... | collective-permute-start | bytes 61448 | tf_op jit(solution)/shard_map/ppermute | solution.py:26
  316.6 22.3 %all-to-all-start.2 = ((f32[256,4,128]{2,1,0:T(4,128)}), f32[256,4,128]{2,1,0:T(4,128)S(1)}, u32[]{:S(2)}, u32[]{:S(2)}) async-start(f32[256,4,128]{2,1,0:T(4,128)} %broadcast_select_fusion), calls=%async_computation.2 | async-start | bytes 1048576 | tf_op jit(solution)/shard_map/all_to_all | solution.py:179
  325.0 0.7 copy-start.1
where the time goes:
time: 341 us; the launch traced here: 340 us
  other arithmetic  145 us (43%)
  starting transfers between devices  96.6 us (28%)
  waiting for transfers between devices  55.9 us (16%)
  local copies, waits for them, and re-layouts  32.7 us (10%)
  loops' own time  8.24 us (2%)
    reduce_sum x27, other arithmetic, pair_block(): jnp.sum(coupling * delta_x, axis=-2)  82.2 us
    reduce_sum x27, other arithmetic, pair_block(): far_sum = jnp.sum(kernel * own_wt, axis=-2)  50.1 us
    ppermute x12, starting transfers between devices, with_halo(): lax.ppermute(tail, axis, [(i, (i + 1) % count) for i in range(ends)])  47 us
    ppermute x12, waiting for transfers between devices, with_halo(): lax.ppermute(head, axis, [((i + 1) % count, i) for i in range(ends)])  32.6 us
    ppermute x12, starting transfers between devices, with_halo(): lax.ppermute(head, axis, [((i + 1) % count, i) for i in range(ends)])  18.8 us
    all_to_all x1, waiting for transfers between devices, on_device(): lax.all_to_all(reply_rows, ('gx', 'gy', 'gz'), split_axis=0, concat_axis=...  12.4 us
    all_to_all x1, starting transfers between devices, on_device(): lax.all_to_all(labels, ('gx', 'gy', 'gz'), split_axis=0, concat_axis=0, t...  11.5 us
    all_to_all x1, starting transfers between devices, on_device(): lax.all_to_all(outgoing, ('gx', 'gy', 'gz'), split_axis=0, concat_axis=0,...  11 us
  transfers between devices with their start and end apart: 27, of which 14 were waited for; matrix products, arithmetic and copies ran while one was open for 5% of the time, Pallas kernels for 0%

commit v1 on v0

v1 whole, which is shorter than its diff:
```python
import functools
import math

import jax
import jax.numpy as jnp
from jax import lax
from jax.experimental import pallas as pl
from jax.experimental.pallas import tpu as pltpu
from jax.sharding import PartitionSpec as P

AXES = ("gx", "gy", "gz")
SX, SY, SZ = 8, 4, 4
BRICKS = SX * SY * SZ
CY, CZ = 4, 16
CELLS = CY * CZ
BLOCKS = 48
SLOTS = 32
LANES = 128
QUADS = CZ // 4
CHUNK = 32
GROUPS = CHUNK // 8
PER_CELL = LANES // CHUNK

LOG2E = 1.4426950408889634
WIDTH = 0.05
CUTOFF = 0.5
SHARP = CUTOFF / WIDTH * LOG2E
LIFT = math.log2(SHARP)
SCALE = math.sqrt(LOG2E / CUTOFF)
BACK = 2.0 / (SHARP * SCALE)
FLOOR = math.exp(-10.0)
GONE = -1.0e4
NUDGE = 4.0e-6

F32 = jnp.float32
I32 = jnp.int32
VMEM = pl.BlockSpec(memory_space=pltpu.VMEM)
SMEM = pl.BlockSpec(memory_space=pltpu.SMEM)
MESH = pl.DeviceIdType.MESH


def iota(shape, dim):
    return lax.broadcasted_iota(I32, shape, dim)


def here():
    return lax.axis_index("gx"), lax.axis_index("gy"), lax.axis_index("gz")


def place_of(brick):
    return (brick // (SY * SZ), brick // SZ % SY, brick % SZ)


def pack_kernel(cell_ref, count_ref, gcount_ref, xyz_ref, weight_ref, mean_ref, opacity_ref,
                out_ref, gauss_ref, slot_ref, used_ref):
    out_ref[...] = jnp.zeros_like(out_ref)

    def clear(i, carry):
        for u in range(8):
            used_ref[i * 8 + u] = 0
        return carry

    lax.fori_loop(0, BRICKS // 8, clear, 0)
    lane = iota((1, LANES), 1)
    row4 = iota((4, LANES), 0)
    lane4 = iota((4, LANES), 1)
    row8 = iota((8, LANES), 0)

    def one(b, carry):
        cell = cell_ref[b]
        cx = cell >> 10
        cy = (cell >> 6) & 15
        cz = cell & 63
        brick = (cx * SY + (cy >> 2)) * SZ + (cz >> 4)
        k = used_ref[brick]
        used_ref[brick] = k + 1
        slot_ref[b] = brick * 2 + k
        weight = jnp.where(lane < count_ref[b], weight_ref[pl.ds(b, 1), :], 0.0)
        rows = jnp.concatenate([xyz_ref[b], weight], axis=0)
        corner = jnp.where(row4 == 0, cx, jnp.where(row4 == 1, cy, cz))
        top = (corner + 1).astype(F32) - NUDGE
        rows = jnp.where((lane4 == 0) & (row4 < 3), jnp.minimum(rows, top), rows)
        both = jnp.concatenate([rows, rows], axis=0)
        out_ref[brick] = jnp.where((row8 >> 2) == k, both, out_ref[brick])
        return carry

    lax.fori_loop(0, BLOCKS, one, 0)
    for y in range(CY):
        for q in range(QUADS):
            mean = jnp.concatenate([mean_ref[y, 4 * q + r] for r in range(4)], axis=1)
            opacity = jnp.concatenate(
                [opacity_ref[y, 4 * q + r : 4 * q + r + 1, :] for r in range(4)], axis=1
            )
            base = y * CZ + 4 * q
            count = jnp.where(
                lane < 64,
                jnp.where(lane < 32, gcount_ref[base], gcount_ref[base + 1]),
                jnp.where(lane < 96, gcount_ref[base + 2], gcount_ref[base + 3]),
            )
            opacity = jnp.where((lane & 31) < count, opacity, 0.0)
            gauss_ref[y, q] = jnp.concatenate([mean, opacity, jnp.zeros((4, LANES), F32)], axis=0)


def pack(block_cell, block_count, gauss_count, xyz, weight, mean, opacity):
    return pl.pallas_call(
        pack_kernel,
        out_shape=(
            jax.ShapeDtypeStruct((BRICKS, 8, LANES), F32),
            jax.ShapeDtypeStruct((CY, QUADS, 8, LANES), F32),
            jax.ShapeDtypeStruct((BLOCKS,), I32),
        ),
        in_specs=[SMEM, SMEM, SMEM, VMEM, VMEM, VMEM, VMEM],
        out_specs=(VMEM, VMEM, SMEM),
        scratch_shapes=[pltpu.SMEM((BRICKS,), I32)],
        name="pack",
    )(block_cell, block_count, gauss_count, xyz, weight, mean, opacity)


OFFSETS = [
    (ox, oy, oz)
    for ox in (-1, 0, 1)
    for oy in (-1, 0, 1)
    for oz in (-1, 0, 1)
    if (ox, oy, oz) != (0, 0, 0)
]
OFFSETS.sort(key=lambda o: abs(o[1]) + abs(o[2]))


def neighbour(offset):
    gx, gy, gz = here()
    ox, oy, oz = offset
    return ((gx + ox + SX) % SX, (gy + oy + SY) % SY, (gz + oz + SZ) % SZ)


def greet_all():
    gx, gy, gz = here()
    me = (gx * SY + gy) * SZ + gz
    barrier = pltpu.get_barrier_semaphore()

    def signal(i, carry):
        pl.semaphore_signal(barrier, inc=1, device_id=place_of((me + i) % BRICKS), device_id_type=MESH)
        return carry

    lax.fori_loop(1, BRICKS, signal, 0)
    pl.semaphore_wait(barrier, BRICKS - 1)


def greet_near():
    barrier = pltpu.get_barrier_semaphore()
    for offset in OFFSETS:
        pl.semaphore_signal(barrier, inc=1, device_id=neighbour(offset), device_id_type=MESH)
    pl.semaphore_wait(barrier, len(OFFSETS))


def exchange_copy(src_ref, dst_ref, send_sem, recv_sem, i):
    gx, gy, gz = here()
    me = (gx * SY + gy) * SZ + gz
    peer = (me + i) % BRICKS
    return pltpu.make_async_remote_copy(
        src_ref=src_ref.at[peer],
        dst_ref=dst_ref.at[me],
        send_sem=send_sem.at[i],
        recv_sem=recv_sem.at[i],
        device_id=place_of(peer),
        device_id_type=MESH,
    )


def exchange_start(*refs):
    def step(i, carry):
        exchange_copy(*refs, i).start()
        return carry

    lax.fori_loop(1, BRICKS, step, 0)


def exchange_wait(*refs):
    def step(i, carry):
        exchange_copy(*refs, i).wait()
        return carry

    lax.fori_loop(1, BRICKS, step, 0)


def send_kernel(out_ref, gauss_ref, in_ref, halo_ref, asend, arecv, hsend, hrecv):
    gx, gy, gz = here()
    me = (gx * SY + gy) * SZ + gz
    greet_all()
    copies = []
    for d, (ox, oy, oz) in enumerate(OFFSETS):
        sy, ty, ny = (0, 1, CY) if oy == 0 else ((CY - 1, 0, 1) if oy > 0 else (0, CY + 1, 1))
        sq, tq, nq = (0, 1, QUADS) if oz == 0 else ((QUADS - 1, 0, 1) if oz > 0 else (0, QUADS + 1, 1))
        copies.append(
            pltpu.make_async_remote_copy(
                src_ref=gauss_ref.at[pl.ds(sy, ny), pl.ds(sq, nq)],
                dst_ref=halo_ref.at[1 - ox, pl.ds(ty, ny), pl.ds(tq, nq)],
                send_sem=hsend.at[d],
                recv_sem=hrecv.at[d],
                device_id=neighbour((ox, oy, oz)),
                device_id_type=MESH,
            )
        )
    exchange_start(out_ref, in_ref, asend, arecv)
    for copy in copies:
        copy.start()
    in_ref[me] = out_ref[me]
    for y in range(CY):
        for q in range(QUADS):
            halo_ref[1, y + 1, q + 1] = gauss_ref[y, q]
    for copy in copies:
        copy.wait()
    exchange_wait(out_ref, in_ref, asend, arecv)


def send(outgoing, gauss):
    return pl.pallas_call(
        send_kernel,
        out_shape=(
            jax.ShapeDtypeStruct((BRICKS, 8, LANES), F32),
            jax.ShapeDtypeStruct((3, CY + 2, QUADS + 2, 8, LANES), F32),
        ),
        in_specs=[VMEM, VMEM],
        out_specs=(VMEM, VMEM),
        scratch_shapes=[
            pltpu.SemaphoreType.DMA((BRICKS,)),
            pltpu.SemaphoreType.DMA((BRICKS,)),
            pltpu.SemaphoreType.DMA((26,)),
            pltpu.SemaphoreType.DMA((26,)),
        ],
        compiler_params=pltpu.CompilerParams(collective_id=0, has_side_effects=True),
        name="send",
    )(outgoing, gauss)


def spread(row):
    return jnp.broadcast_to(row, (8, LANES))


def first_kernel(in_ref, halo_ref, pts_ref, win_ref, part_ref, items_ref, slots_ref, total_ref,
                 meta_ref, metas_ref, turn_ref, zp_ref, acc_ref, sem):
    gx, gy, gz = here()
    row8 = iota((8, LANES), 0)
    lane8 = iota((8, LANES), 1)
    lane1 = iota((1, LANES), 1)

    def gather(i, found):
        for u in range(16):
            s = i * 16 + u
            tile = in_ref[s]
            mark = jnp.where((row8 & 3) == 3, (tile > 0.0).astype(F32), jnp.where(lane8 == 0, tile, 0.0))
            found = jnp.where(lane8 == s, jnp.sum(mark, axis=1, keepdims=True), found)
        return found

    found = lax.fori_loop(0, BRICKS // 16, gather, jnp.zeros((8, LANES), F32))
    cell = iota((CELLS, LANES), 0).astype(F32)
    lane64 = iota((CELLS, LANES), 1).astype(F32)
    slot = jnp.full((CELLS, LANES), -1.0, F32)
    count = jnp.zeros((CELLS, LANES), F32)
    for k in range(2):
        y0 = jnp.floor(found[4 * k + 1 : 4 * k + 2]) - (gy * CY).astype(F32)
        z0 = jnp.floor(found[4 * k + 2 : 4 * k + 3]) - (gz * CZ).astype(F32)
        size = found[4 * k + 3 : 4 * k + 4]
        label = jnp.where(size > 0.0, y0 * CZ + z0, -1.0)
        match = label == cell
        slot = jnp.where(match, 2.0 * lane64 + k, slot)
        count = jnp.where(match, jnp.broadcast_to(size, (CELLS, LANES)), count)
    slot = jnp.max(slot, axis=1, keepdims=True)
    count = jnp.max(count, axis=1, keepdims=True)
    meta_ref[...] = jnp.where(iota((CELLS, LANES), 1) == 0, slot, count).astype(I32)
    copy = pltpu.make_async_copy(meta_ref, metas_ref, sem)
    copy.start()

    acc_ref[...] = jnp.zeros_like(acc_ref)
    origin = jnp.where(row8 == 0, gx, jnp.where(row8 == 1, gy * CY + CY // 2, gz * CZ)).astype(F32)
    origin = jnp.where(row8 < 3, origin, 0.0)
    scale = jnp.where(row8 < 3, SCALE, 1.0).astype(F32)

    def windows(xy, carry):
        x = xy // (CY + 2)
        y = xy % (CY + 2)
        outside = ((x == 0) & (gx == 0)) | ((x == 2) & (gx == SX - 1))
        outside = outside | ((y == 0) & (gy == 0)) | ((y == CY + 1) & (gy == SY - 1))
        tiles = []
        for q in range(QUADS + 2):
            gone = outside
            if q == 0:
                gone = gone | (gz == 0)
            if q == QUADS + 1:
                gone = gone | (gz == SZ - 1)
            tile = halo_ref[x, y, q]
            opacity = jnp.where(gone, 0.0, tile)
            strength = jnp.where(opacity > 0.0, jnp.log2(jnp.maximum(opacity, 1e-30)) - SHARP, GONE)
            tiles.append(jnp.where(row8 == 3, strength, (tile - origin) * scale))
        for z in range(CZ):
            a, b = z // 4, z % 4
            if b == 0:
                tile = pltpu.roll(jnp.where(lane8 >= 96, tiles[a], tiles[a + 1]), 32, 1)
            elif b == 1:
                tile = tiles[a + 1]
            elif b == 2:
                tile = pltpu.roll(tiles[a + 1], 96, 1)
            else:
                tile = pltpu.roll(jnp.where(lane8 < 64, tiles[a + 2], tiles[a + 1]), 64, 1)
            tile = jnp.where((row8 == 3) & (lane8 >= 96), GONE, tile)
            tile = jnp.where(row8 == 2, tile - z * SCALE, tile)
            win_ref[z, xy] = tile
        return carry

    lax.fori_loop(0, 3 * (CY + 2), windows, 0)
    copy.wait()

    def listing(c, at):
        size = metas_ref[c, 1]
        slots_ref[c] = metas_ref[c, 0]
        for u in range(PER_CELL):
            items_ref[at + u] = c * PER_CELL + u
        return at + ((size + CHUNK - 1) >> (CHUNK.bit_length() - 1))

    total = lax.fori_loop(0, CELLS, listing, 0)
    total_ref[0] = total

    def prepare(i, carry):
        for u in range(4):
            c = i * 4 + u
            slot = slots_ref[c]
            safe = jnp.maximum(slot, 0)
            tile = in_ref[safe >> 1]
            tile = jnp.where((safe & 1) == 1, pltpu.roll(tile, 4, 0), tile)
            tile = jnp.where(slot >= 0, tile, 0.0)
            z = (c & (CZ - 1)).astype(F32)
            shift = origin + jnp.where(row8 == 2, z, 0.0)
            weight = jnp.where(tile > 0.0, jnp.log2(jnp.maximum(tile, 1e-30)), GONE)
            points = jnp.where(row8 == 3, weight, (tile - shift) * scale)
            points = jnp.where(row8 == 4, pltpu.roll(tile, 1, 0), points)
            pts_ref[c] = points
            turn_ref[c] = jnp.transpose(points)
        return carry

    lax.fori_loop(0, CELLS // 4, prepare, 0)

    def sweep(i, carry):
        item = items_ref[i]
        c = item >> (PER_CELL.bit_length() - 1)
        first = (item & (PER_CELL - 1)) * CHUNK
        y = c >> 4
        z = c & (CZ - 1)
        cols = [turn_ref[c, pl.ds(pl.multiple_of(first + 8 * g, 8), 8), :] for g in range(GROUPS)]
        feats = [[jnp.broadcast_to(col[:, f : f + 1], (8, LANES)) for f in range(4)] for col in cols]
        sums = [jnp.zeros((8, LANES), F32) for g in range(GROUPS)]
        for dx in range(3):
            for dy in range(3):
                xy = dx * (CY + 2) + y + dy
                mx, my, mz, la = [spread(win_ref[z, xy, f : f + 1, :]) for f in range(4)]
                far = None
                for g in range(GROUPS):
                    px, py, pz, lw = feats[g]
                    ex, ey, ez = px - mx, py - my, pz - mz
                    fall = jnp.exp2(LIFT - ex * ex - ey * ey - ez * ez)
                    term = jnp.exp2(fall + (la + lw))
                    sums[g] = sums[g] + term
                    far = term if far is None else far + term
                acc_ref[z, xy] = acc_ref[z, xy] + far
        for g in range(GROUPS):
            zp_ref[c, pl.ds(pl.multiple_of(first + 8 * g, 8), 8), :] = sums[g]
        return carry

    lax.fori_loop(0, total, sweep, 0)

    def fold(xy, carry):
        part_ref[xy] = fold_quads([acc_ref[z, xy] for z in range(CZ)], lane8)
        return carry

    lax.fori_loop(0, 3 * (CY + 2), fold, 0)

    def finish(i, carry):
        for u in range(4):
            c = i * 4 + u
            tile = pts_ref[c]
            weight = tile[4:5]
            valid = weight > 0.0
            density = jnp.sum(jnp.transpose(zp_ref[c]), axis=0, keepdims=True)
            total_p = FLOOR + jnp.where(valid, density / jnp.where(valid, weight, 1.0), 0.0)
            inverse = jnp.where(valid, 1.0 / total_p, 0.0)
            loss = jnp.where(valid, -WIDTH * jnp.log(total_p), 0.0)
            tile = jnp.where(row8 == 4, inverse, tile)
            pts_ref[c] = jnp.where(row8 == 5, loss, tile)
        return carry

    lax.fori_loop(0, CELLS // 4, finish, 0)


def fold_quads(tiles, lane8):
    quads = [jnp.zeros((8, LANES), F32) for q in range(QUADS + 2)]
    for z, tile in enumerate(tiles):
        a, b = z // 4, z % 4
        if b == 1:
            quads[a + 1] = quads[a + 1] + tile
        elif b == 2:
            quads[a + 1] = quads[a + 1] + pltpu.roll(tile, 32, 1)
        elif b == 0:
            moved = pltpu.roll(tile, 96, 1)
            quads[a] = quads[a] + jnp.where(lane8 >= 96, moved, 0.0)
            quads[a + 1] = quads[a + 1] + jnp.where(lane8 < 96, moved, 0.0)
        else:
            moved = pltpu.roll(tile, 64, 1)
            quads[a + 1] = quads[a + 1] + jnp.where(lane8 >= 64, moved, 0.0)
            quads[a + 2] = quads[a + 2] + jnp.where(lane8 < 64, moved, 0.0)
    rows = [jnp.sum(quad, axis=0, keepdims=True) for quad in quads]
    return jnp.concatenate(rows + [jnp.zeros((2, LANES), F32)], axis=0)


def first_sweep(incoming, halo):
    return pl.pallas_call(
        first_kernel,
        out_shape=(
            jax.ShapeDtypeStruct((CELLS, 8, LANES), F32),
            jax.ShapeDtypeStruct((CZ, 18, 8, LANES), F32),
            jax.ShapeDtypeStruct((18, 8, LANES), F32),
            jax.ShapeDtypeStruct((CELLS * PER_CELL + 8,), I32),
            jax.ShapeDtypeStruct((CELLS,), I32),
            jax.ShapeDtypeStruct((1,), I32),
        ),
        in_specs=[VMEM, VMEM],
        out_specs=(VMEM, VMEM, VMEM, SMEM, SMEM, SMEM),
        scratch_shapes=[
            pltpu.VMEM((CELLS, LANES), I32),
            pltpu.SMEM((CELLS, LANES), I32),
            pltpu.VMEM((CELLS, LANES, 8), F32),
            pltpu.VMEM((CELLS, LANES, LANES), F32),
            pltpu.VMEM((CZ, 18, 8, LANES), F32),
            pltpu.SemaphoreType.DMA,
        ],
        compiler_params=pltpu.CompilerParams(vmem_limit_bytes=48 * 1024 * 1024),
        name="first_sweep",
    )(incoming, halo)


def near_copies(part_of, box_ref, send_sem, recv_sem):
    copies = []
    for d, (ox, oy, oz) in enumerate(OFFSETS):
        y0, ny = (1, CY) if oy == 0 else ((CY + 1, 1) if oy > 0 else (0, 1))
        copies.append(
            pltpu.make_async_remote_copy(
                src_ref=part_of((1 + ox) * (CY + 2) + y0, ny),
                dst_ref=box_ref.at[d, pl.ds(0, ny)],
                send_sem=send_sem.at[d],
                recv_sem=recv_sem.at[d],
                device_id=neighbour((ox, oy, oz)),
                device_id_type=MESH,
            )
        )
    return copies


def quads_of(tile, oz):
    if oz == 0:
        return tile[1 : QUADS + 1]
    row = iota((QUADS, LANES), 0)
    if oz > 0:
        return jnp.where(row == 0, tile[QUADS + 1 : QUADS + 2], 0.0)
    return jnp.where(row == QUADS - 1, tile[0:1], 0.0)


def middle_kernel(part_ref, gauss_ref, inv_ref, loss_ref, box_ref, send1, recv1, send2, recv2):
    greet_near()
    copies = near_copies(lambda at, n: part_ref.at[pl.ds(at, n)], box_ref, send1, recv1)
    for copy in copies:
        copy.start()
    sums = [part_ref[(CY + 2) + y + 1][1 : QUADS + 1] for y in range(CY)]
    for d, (ox, oy, oz) in enumerate(OFFSETS):
        copies[d].wait_recv()
        for k in range(CY if oy == 0 else 1):
            y = k if oy == 0 else (0 if oy > 0 else CY - 1)
            sums[y] = sums[y] + quads_of(box_ref[d, k], oz)
    for y in range(CY):
        opacity = jnp.concatenate([gauss_ref[y, q][3:4] for q in range(QUADS)], axis=0)
        valid = opacity > 0.0
        total_g = FLOOR + jnp.where(valid, sums[y] / jnp.where(valid, opacity, 1.0), 0.0)
        blank = jnp.zeros((8 - QUADS, LANES), F32)
        inv_ref[1, (CY + 2) + y + 1] = jnp.concatenate([1.0 / total_g, blank], axis=0)
        loss = jnp.where(valid, -WIDTH * jnp.log(total_g), 0.0)
        loss_ref[y] = jnp.concatenate([loss, opacity], axis=0)
    back = []
    for d, (ox, oy, oz) in enumerate(OFFSETS):
        sy, ty, ny = (0, 1, CY) if oy == 0 else ((CY - 1, 0, 1) if oy > 0 else (0, CY + 1, 1))
        back.append(
            pltpu.make_async_remote_copy(
                src_ref=inv_ref.at[1, pl.ds((CY + 2) + 1 + sy, ny)],
                dst_ref=inv_ref.at[1 - oz, pl.ds((1 - ox) * (CY + 2) + ty, ny)],
                send_sem=send2.at[d],
                recv_sem=recv2.at[d],
                device_id=neighbour((ox, oy, oz)),
                device_id_type=MESH,
            )
        )
    for copy in back:
        copy.start()
    for copy in copies:
        copy.wait_send()
    for copy in back:
        copy.wait()


def middle(part, gauss):
    return pl.pallas_call(
        middle_kernel,
        out_shape=(
            jax.ShapeDtypeStruct((3, 18, 8, LANES), F32),
            jax.ShapeDtypeStruct((CY, 8, LANES), F32),
        ),
        in_specs=[VMEM, VMEM],
        out_specs=(VMEM, VMEM),
        scratch_shapes=[pltpu.VMEM((26, CY, 8, LANES), F32)] + [pltpu.SemaphoreType.DMA((26,))] * 4,
        compiler_params=pltpu.CompilerParams(collective_id=1, has_side_effects=True),
        name="middle",
    )(part, gauss)


def second_kernel(items_ref, slots_ref, total_ref, pts_ref, win_ref, inv_ref, reply_ref, part_ref,
                  turn_ref, ig_ref, grad_ref, acc_ref):
    row8 = iota((8, LANES), 0)
    lane8 = iota((8, LANES), 1)
    lane1 = iota((1, LANES), 1)
    reply_ref[...] = jnp.zeros_like(reply_ref)
    acc_ref[...] = jnp.zeros_like(acc_ref)

    def windows(xy, carry):
        own = inv_ref[1, xy]
        rows = [inv_ref[0, xy][QUADS - 1 : QUADS]] + [own[q : q + 1] for q in range(QUADS)]
        tile = jnp.concatenate(rows + [inv_ref[2, xy][0:1], jnp.zeros((2, LANES), F32)], axis=0)
        moved = [pltpu.roll(tile, 32, 1), tile, pltpu.roll(tile, 96, 1), pltpu.roll(tile, 64, 1)]
        for z in range(CZ):
            a, b = z // 4, z % 4
            row = moved[b][a + 1 : a + 2]
            if b == 0:
                row = jnp.where(lane1 < 32, moved[b][a : a + 1], row)
            elif b == 3:
                row = jnp.where(lane1 >= 64, moved[b][a + 2 : a + 3], row)
            ig_ref[z, xy] = spread(row)
        return carry

    lax.fori_loop(0, 18, windows, 0)

    def prepare(i, carry):
        for u in range(4):
            turn_ref[i * 4 + u] = jnp.transpose(pts_ref[i * 4 + u])
        return carry

    lax.fori_loop(0, CELLS // 4, prepare, 0)

    def sweep(i, carry):
        item = items_ref[i]
        c = item >> (PER_CELL.bit_length() - 1)
        first = (item & (PER_CELL - 1)) * CHUNK
        y = c >> 4
        z = c & (CZ - 1)
        cols = [turn_ref[c, pl.ds(pl.multiple_of(first + 8 * g, 8), 8), :] for g in range(GROUPS)]
        feats = [[jnp.broadcast_to(col[:, f : f + 1], (8, LANES)) for f in range(5)] for col in cols]
        sums = [[jnp.zeros((8, LANES), F32) for k in range(3)] for g in range(GROUPS)]
        for dx in range(3):
            for dy in range(3):
                xy = dx * (CY + 2) + y + dy
                mx, my, mz, la = [spread(win_ref[z, xy, f : f + 1, :]) for f in range(4)]
                ig = ig_ref[z, xy]
                far = [None] * 4
                for g in range(GROUPS):
                    px, py, pz, lw, ip = feats[g]
                    ex, ey, ez = px - mx, py - my, pz - mz
                    fall = jnp.exp2(LIFT - ex * ex - ey * ey - ez * ez)
                    term = jnp.exp2(fall + (la + lw))
                    pull = (term * fall) * (ip + ig)
                    parts = [pull * ex, pull * ey, pull * ez, term * ip]
                    for k in range(3):
                        sums[g][k] = sums[g][k] + parts[k]
                    far = [p if f is None else f + p for f, p in zip(far, parts)]
                for k in range(4):
                    acc_ref[z, xy, k] = acc_ref[z, xy, k] + far[k]
        for g in range(GROUPS):
            for k in range(3):
                grad_ref[k, c, pl.ds(pl.multiple_of(first + 8 * g, 8), 8), :] = sums[g][k]
        return carry

    lax.fori_loop(0, total_ref[0], sweep, 0)

    def fold(xy, carry):
        for k in range(4):
            part_ref[xy, k] = fold_quads([acc_ref[z, xy, k] for z in range(CZ)], lane8)
        return carry

    lax.fori_loop(0, 18, fold, 0)

    def finish(i, carry):
        for u in range(2):
            c = i * 2 + u
            tile = pts_ref[c]
            valid = tile[3:4] > 0.5 * GONE
            rows = [
                jnp.where(valid, jnp.sum(jnp.transpose(grad_ref[k, c]), axis=0, keepdims=True) * BACK, 0.0)
                for k in range(3)
            ]
            out = jnp.concatenate([tile[5:6]] + rows, axis=0)
            out = jnp.concatenate([out, out], axis=0)
            slot = slots_ref[c]
            safe = jnp.maximum(slot, 0)
            keep = ((row8 >> 2) == (safe & 1)) & (slot >= 0)
            reply_ref[safe >> 1] = jnp.where(keep, out, reply_ref[safe >> 1])
        return carry

    lax.fori_loop(0, CELLS // 2, finish, 0)


def second_sweep(items, slots, total, pts, win, inv):
    return pl.pallas_call(
        second_kernel,
        out_shape=(
            jax.ShapeDtypeStruct((BRICKS, 8, LANES), F32),
            jax.ShapeDtypeStruct((18, 4, 8, LANES), F32),
        ),
        in_specs=[SMEM, SMEM, SMEM, VMEM, VMEM, VMEM],
        out_specs=(VMEM, VMEM),
        scratch_shapes=[
            pltpu.VMEM((CELLS, LANES, 8), F32),
            pltpu.VMEM((CZ, 18, 8, LANES), F32),
            pltpu.VMEM((3, CELLS, LANES, LANES), F32),
            pltpu.VMEM((CZ, 18, 4, 8, LANES), F32),
        ],
        compiler_params=pltpu.CompilerParams(vmem_limit_bytes=56 * 1024 * 1024),
        name="second_sweep",
    )(items, slots, total, pts, win, inv)


def last_kernel(reply_ref, part_ref, loss_ref, ans_ref, grad_ref, box_ref, asend, arecv, hsend, hrecv):
    gx, gy, gz = here()
    me = (gx * SY + gy) * SZ + gz
    greet_all()
    copies = near_copies(lambda at, n: part_ref.at[pl.ds(at, n)], box_ref, hsend, hrecv)
    for copy in copies:
        copy.start()
    exchange_start(reply_ref, ans_ref, asend, arecv)
    ans_ref[me] = reply_ref[me]
    sums = [[part_ref[(CY + 2) + y + 1, k][1 : QUADS + 1] for k in range(4)] for y in range(CY)]
    for d, (ox, oy, oz) in enumerate(OFFSETS):
        copies[d].wait_recv()
        for j in range(CY if oy == 0 else 1):
            y = j if oy == 0 else (0 if oy > 0 else CY - 1)
            for k in range(4):
                sums[y][k] = sums[y][k] + quads_of(box_ref[d, j, k], oz)
    for y in range(CY):
        loss = loss_ref[y][0:QUADS]
        opacity = loss_ref[y][QUADS : 2 * QUADS]
        valid = opacity > 0.0
        for k in range(3):
            grad_ref[y, k] = jnp.where(valid, sums[y][k] * (-BACK), 0.0)
        dense = sums[y][3] / jnp.where(valid, opacity, 1.0)
        grad_ref[y, 3] = jnp.where(valid, loss - WIDTH * dense, 0.0)
    for copy in copies:
        copy.wait_send()
    exchange_wait(reply_ref, ans_ref, asend, arecv)


def last(reply, part, loss):
    return pl.pallas_call(
        last_kernel,
        out_shape=(
            jax.ShapeDtypeStruct((BRICKS, 8, LANES), F32),
            jax.ShapeDtypeStruct((CY, 4, QUADS, LANES), F32),
        ),
        in_specs=[VMEM, VMEM, VMEM],
        out_specs=(VMEM, VMEM),
        scratch_shapes=[
            pltpu.VMEM((26, CY, 4, 8, LANES), F32),
            pltpu.SemaphoreType.DMA((BRICKS,)),
            pltpu.SemaphoreType.DMA((BRICKS,)),
            pltpu.SemaphoreType.DMA((26,)),
            pltpu.SemaphoreType.DMA((26,)),
        ],
        compiler_params=pltpu.CompilerParams(collective_id=2, has_side_effects=True),
        name="last",
    )(reply, part, loss)


def place_kernel(slot_ref, ans_ref, grad_ref, point_ref, gauss_ref):
    def one(b, carry):
        slot = slot_ref[b]
        tile = ans_ref[slot >> 1]
        tile = jnp.where((slot & 1) == 1, pltpu.roll(tile, 4, 0), tile)
        point_ref[b] = tile[0:4]
        return carry

    lax.fori_loop(0, BLOCKS, one, 0)
    for y in range(CY):
        rows = [grad_ref[y, k] for k in range(4)]
        for q in range(QUADS):
            tile = jnp.concatenate([row[q : q + 1] for row in rows], axis=0)
            for r in range(4):
                gauss_ref[0, y, 4 * q + r] = tile[:, SLOTS * r : SLOTS * r + SLOTS]


def place(slots, answer, grad):
    return pl.pallas_call(
        place_kernel,
        out_shape=(
            jax.ShapeDtypeStruct((BLOCKS, 4, LANES), F32),
            jax.ShapeDtypeStruct((1, CY, CZ, 4, SLOTS), F32),
        ),
        in_specs=[SMEM, VMEM, VMEM],
        out_specs=(VMEM, VMEM),
        name="place",
    )(slots, answer, grad)


def on_device(point_xyz, point_weight, block_cell, block_count, gauss_mean, gauss_opacity, gauss_count):
    outgoing, gauss, slots = pack(
        block_cell,
        block_count,
        gauss_count.reshape(CELLS),
        point_xyz,
        point_weight,
        gauss_mean.reshape(CY, CZ, 3, SLOTS),
        gauss_opacity.reshape(CY, CZ, SLOTS),
    )
    incoming, halo = send(outgoing, gauss)
    pts, win, part, items, cell_slots, total = first_sweep(incoming, halo)
    inv, loss = middle(part, gauss)
    reply, part = second_sweep(items, cell_slots, total, pts, win, inv)
    answer, grad = last(reply, part, loss)
    return place(slots, answer, grad)


def solution(mesh):
    return jax.shard_map(
        on_device,
        mesh=mesh,
        in_specs=(
            P(AXES, None, None),
            P(AXES, None),
            P(AXES),
            P(AXES),
            P("gx", "gy", "gz", None, None),
            P("gx", "gy", "gz", None),
            P("gx", "gy", "gz"),
        ),
        out_specs=(P(AXES, None, None), P("gx", "gy", "gz", None, None)),
        check_vma=False,
    )
```

time: 341 us -> 179 us (0.52)
  Pallas kernels: 0 us -> 170 us
  other arithmetic: 145 us -> 0 us
  starting transfers between devices: 96.6 us -> 0 us
  waiting for transfers between devices: 55.9 us -> 0 us
  local copies, waits for them, and re-layouts: 32.7 us -> 10 us
  loops' own time: 8.24 us -> 0 us
    pallas_call x0 -> x7, Pallas kernels: none -> 170 us  [the longest x1 39.9 us: last(): pl.pallas_call(last_kernel, out_shape=(jax.ShapeDtypeStruct((BRICKS, 8, L...]
    reduce_sum x55 -> x0, other arithmetic: 132 us -> none  [the longest x27 82.2 us: pair_block(): jnp.sum(coupling * delta_x, axis=-2)]
    ppermute x24 -> x0, starting transfers between devices: 65.8 us -> none  [the longest x12 47 us: with_halo(): lax.ppermute(tail, axis, [(i, (i + 1) % count) for i in range(ends)])]
    ppermute x24 -> x0, waiting for transfers between devices: 40.6 us -> none  [the longest x12 32.6 us: with_halo(): lax.ppermute(head, axis, [((i + 1) % count, i) for i in range(ends)])]
    all_to_all x3 -> x0, starting transfers between devices: 30.8 us -> none  [the longest x1 11.5 us: on_device(): lax.all_to_all(labels, ('gx', 'gy', 'gz'), split_axis=0, concat_axis=0, t...]
    all_to_all x3 -> x0, waiting for transfers between devices: 15.3 us -> none  [the longest x1 12.4 us: on_device(): lax.all_to_all(reply_rows, ('gx', 'gy', 'gz'), split_axis=0, concat_axis=...]
    scatter x3 -> x0, local copies, waits for them, and re-layouts: 13.4 us -> none  [the longest x1 7.62 us: on_device(): jnp.zeros((cell_total, 4, points_len), jnp.float32).at[placed]]
    dynamic_update_slice x54 -> x0, local copies, waits for them, and re-layouts: 11 us -> none  [put_window(): return lax.dynamic_update_slice(values, update, corner)]
  transfers between devices with their start and end apart: 27 -> 0, of which waited for: 14 -> 0; matrix products, arithmetic and copies ran while one was open for 5% -> 0% of each run, Pallas kernels for 0% -> 0%
where the time goes in v1:
time: 179 us; the launch traced here: 181 us
  Pallas kernels  170 us (95%)
  local copies, waits for them, and re-layouts  10 us (6%)
    pallas_call x1, Pallas kernels, last(): pl.pallas_call(last_kernel, out_shape=(jax.ShapeDtypeStruct((BRICKS, 8, L...  39.9 us
    pallas_call x1, Pallas kernels, second_sweep(): pl.pallas_call(second_kernel, out_shape=(jax.ShapeDtypeStruct((BRICKS, 8,...  39.3 us
    pallas_call x1, Pallas kernels, send(): pl.pallas_call(send_kernel, out_shape=(jax.ShapeDtypeStruct((BRICKS, 8, L...  32.8 us
    pallas_call x1, Pallas kernels, first_sweep(): pl.pallas_call(first_kernel, out_shape=(jax.ShapeDtypeStruct((CELLS, 8, L...  28.2 us
    pallas_call x1, Pallas kernels, middle(): pl.pallas_call(middle_kernel, out_shape=(jax.ShapeDtypeStruct((3, 18, 8,...  25.1 us
    unnamed x16, local copies, waits for them, and re-layouts  8.71 us

profile of v1, /device:TPU:1, one launch (start us, length us, event | category | flops | bytes accessed | tf_op | source)
XLA Modules:
  0.0 181.1 jit_solution(17524477179811111552)
XLA Ops:
  0.6 1.3 reshape.13.gcount_ref
  1.9 1.6 copy.10.xyz_ref
  3.5 1.6 copy.12
  5.1 2.8 %pack.1 = (f32[128,8,128]{2,1,0:T(8,128)}, f32[4,4,8,128]{3,2,1,0:T(8,128)}, s32[48]{0:T(128)}) custom-call(s32[48]{0:T(128)} %cell_ref.1, s32[48]{0:T(128)} %count_ref.1, s32[64]{0:T(128)} %reshape.13.gcount_ref, f32[48,3,128]{2,1,0:T(4,128)} %copy.10.xyz_ref, f32[48,128]{1,0:T(8,128)} %weight_ref.1, f32[4,16,3,32]{3,2,1,0:T(4,128)} %bitcast.4, ...), custom_call_target="tpu_custom_call" | custom-call | tf_op jit(solution)/shard_map/pack/pallas_call | solution.py:105
  7.9 32.8 %send.1 = (f32[128,8,128]{2,1,0:T(8,128)}, f32[3,6,6,8,128]{4,3,2,1,0:T(8,128)}) custom-call(f32[128,8,128]{2,1,0:T(8,128)} %get-tuple-element.20.out_ref, f32[4,4,8,128]{3,2,1,0:T(8,128)} %get-tuple-element.21.gauss_ref), custom_call_target="tpu_custom_call" | custom-call | tf_op jit(solution)/shard_map/send/pallas_call | solution.py:216
  40.7 0.0 copy-start.1
  40.7 1.0 copy-done.1
  41.8 0.0 copy-start.2
  41.8 1.0 copy-done.2
  42.8 28.2 %first_sweep.1 = (f32[64,8,128]{2,1,0:T(8,128)S(1)}, f32[16,18,8,128]{3,2,1,0:T(8,128)S(1)}, f32[18,8,128]{2,1,0:T(8,128)S(1)}, s32[264]{0:T(512)S(1)}, s32[64]{0:T(128)S(1)}, /*index=5*/s32[1]{0:T(128)}) custom-call(f32[128,8,128]{2,1,0:T(8,128)S(1)} %copy-done.1, f32[3,6,6,8,128]{4,3,2,1,0:T(8,128)S(1)} %copy-done.2), custom_call_target="tpu_custom_call" | custom-call | tf_op jit(solution)/shard_map/first_sweep/pallas_call | solution.py:413
  71.0 0.0 copy-start
  71.0 1.0 copy-done
  72.0 0.0 copy-start.3
  72.0 0.7 copy-done.3
  72.7 0.0 copy-start.4
  72.7 0.6 copy-done.4
  73.4 0.0 copy-start.5
  73.4 0.6 copy-done.5
  73.9 0.0 copy-start.6
  73.9 0.6 copy-done.6
  74.5 25.1 %middle.1 = (f32[3,18,8,128]{3,2,1,0:T(8,128)}, f32[4,8,128]{2,1,0:T(8,128)}) custom-call(f32[18,8,128]{2,1,0:T(8,128)} %copy-done.4, f32[4,4,8,128]{3,2,1,0:T(8,128)} %get-tuple-element.21.gauss_ref), custom_call_target="tpu_custom_call" | custom-call | tf_op jit(solution)/shard_map/middle/pallas_call | solution.py:505
  99.6 39.3 %second_sweep.1 = (f32[128,8,128]{2,1,0:T(8,128)}, f32[18,4,8,128]{3,2,1,0:T(8,128)}) custom-call(s32[264]{0:T(512)} %copy-done.5, s32[64]{0:T(128)} %copy-done.6, s32[1]{0:T(128)} %get-tuple-element.26.total_ref, f32[64,8,128]{2,1,0:T(8,128)} %copy-done.3, f32[16,18,8,128]{3,2,1,0:T(8,128)} %copy-done, f32[3,18,8,128]{3,2,1,0:T(8,128)} %get-tuple-element.30.inv_ref), custom_call_target="tpu_custom_call" | custom-call | tf_op jit(solution)/shard_map/second_sweep/pallas_call | solution.py:613
  138.9 39.9 %last.1 = (f32[128,8,128]{2,1,0:T(8,128)}, f32[4,4,4,128]{3,2,1,0:T(4,128)}) custom-call(f32[128,8,128]{2,1,0:T(8,128)} %get-tuple-element.31.reply_ref, f32[18,4,8,128]{3,2,1,0:T(8,128)} %get-tuple-element.32.part_ref, f32[4,8,128]{2,1,0:T(8,128)} %get-tuple-element.33.loss_ref), custom_call_target="tpu_custom_call" | custom-call | tf_op jit(solution)/shard_map/last/pallas_call | solution.py:662
  178.9 2.2 %place.1 = (f32[48,4,128]{2,1,0:T(4,128)}, f32[1,4,16,4,32]{4,3,2,1,0:T(4,128)}) custom-call(s32[48]{0:T(128)} %get-tuple-element.19.slot_ref, f32[128,8,128]{2,1,0:T(8,128)} %get-tuple-element.34.ans_ref, f32[4,4,4,128]{3,2,1,0:T(4,128)} %get-tuple-element.35.grad_ref), custom_call_target="tpu_custom_call" | custom-call | tf_op jit(solution)/shard_map/place/pallas_call | solution.py:700
Async XLA Ops:
  40.7 1.0 copy-start.1
  41.8 1.0 copy-start.2
  71.0 1.0 copy-start
  72.0 0.7 copy-start.3
  72.7 0.6 copy-start.4
  73.4 0.6 copy-start.5
  73.9 0.6 copy-start.6

commit v2 on v0

v2 whole, which is shorter than its diff:
```python
import functools
import math

import jax
import jax.numpy as jnp
from jax import lax
from jax.experimental import pallas as pl
from jax.experimental.pallas import tpu as pltpu
from jax.sharding import PartitionSpec as P

AXES = ("gx", "gy", "gz")
SX, SY, SZ = 8, 4, 4
BRICKS = SX * SY * SZ
CY, CZ = 4, 16
CELLS = CY * CZ
BLOCKS = 48
SLOTS = 32
LANES = 128
QUADS = CZ // 4
GROUPS = 4
CHUNKS = LANES // (8 * GROUPS)
ITEMS = CELLS * CHUNKS
TILES = 7
ROWS = CY + 2
COLUMNS = 3 * ROWS

LOG2E = 1.4426950408889634
WIDTH = 0.05
CUTOFF = 0.5
SHARP = CUTOFF / WIDTH * LOG2E
LIFT = math.log2(SHARP)
SCALE = math.sqrt(LOG2E / CUTOFF)
BACK = 2.0 / (SHARP * SCALE)
FLOOR = math.exp(-10.0)
GONE = -1.0e4
NUDGE = 4.0e-6

F32 = jnp.float32
I32 = jnp.int32
VMEM = pl.BlockSpec(memory_space=pltpu.VMEM)
SMEM = pl.BlockSpec(memory_space=pltpu.SMEM)
MESH = pl.DeviceIdType.MESH


def iota(shape, dim):
    return lax.broadcasted_iota(I32, shape, dim)


def here():
    return lax.axis_index("gx"), lax.axis_index("gy"), lax.axis_index("gz")


def place_of(brick):
    return (brick // (SY * SZ), brick // SZ % SY, brick % SZ)


OFFSETS = [
    (ox, oy, oz)
    for ox in (-1, 0, 1)
    for oy in (-1, 0, 1)
    for oz in (-1, 0, 1)
    if (ox, oy, oz) != (0, 0, 0)
]
OFFSETS.sort(key=lambda o: abs(o[1]) + abs(o[2]))


def neighbour(offset):
    gx, gy, gz = here()
    ox, oy, oz = offset
    return ((gx + ox + SX) % SX, (gy + oy + SY) % SY, (gz + oz + SZ) % SZ)


def exchange_copy(src_ref, dst_ref, send_sem, recv_sem, i):
    gx, gy, gz = here()
    me = (gx * SY + gy) * SZ + gz
    peer = (me + i) % BRICKS
    return pltpu.make_async_remote_copy(
        src_ref=src_ref.at[peer],
        dst_ref=dst_ref.at[me],
        send_sem=send_sem.at[i],
        recv_sem=recv_sem.at[i],
        device_id=place_of(peer),
        device_id_type=MESH,
    )


def exchange_start(*refs):
    def step(i, carry):
        exchange_copy(*refs, i).start()
        return carry

    lax.fori_loop(1, BRICKS, step, 0)


def exchange_wait(*refs):
    def step(i, carry):
        exchange_copy(*refs, i).wait()
        return carry

    lax.fori_loop(1, BRICKS, step, 0)


def spread(row):
    return jnp.broadcast_to(row, (8, LANES))


def signal_all():
    gx, gy, gz = here()
    me = (gx * SY + gy) * SZ + gz
    barrier = pltpu.get_barrier_semaphore()

    def signal(i, carry):
        pl.semaphore_signal(barrier, inc=1, device_id=place_of((me + i) % BRICKS), device_id_type=MESH)
        return carry

    lax.fori_loop(1, BRICKS, signal, 0)


def pack_points(cell_ref, count_ref, xyz_ref, weight_ref, pay_ref, out_ref, home_ref, homes_ref, sem):
    lane = iota((1, LANES), 1)
    row4 = iota((4, LANES), 0)
    lane4 = iota((4, LANES), 1)
    row8 = iota((8, LANES), 0)

    def payload(b, carry):
        first, second = carry
        cell = cell_ref[b]
        cx = cell >> 10 & 7
        cy = (cell >> 6) & 15
        cz = cell & 63
        brick = (cx * SY + (cy >> 2)) * SZ + (cz >> 4)
        hit = lane == brick
        later = hit & (first < BLOCKS)
        second = jnp.where(later, b, second)
        first = jnp.where(hit & (first == BLOCKS), b, first)
        weight = jnp.where(lane < count_ref[b], weight_ref[pl.ds(b, 1), :], 0.0)
        rows = jnp.concatenate([xyz_ref[b], weight], axis=0)
        corner = jnp.where(row4 == 0, cx, jnp.where(row4 == 1, cy, cz))
        top = (corner + 1).astype(F32) - NUDGE
        rows = jnp.where((lane4 == 0) & (row4 < 3), jnp.minimum(rows, top), rows)
        pay_ref[b] = jnp.concatenate([rows, rows], axis=0)
        return first, second

    none = jnp.full((1, LANES), BLOCKS, I32)
    first, second = lax.fori_loop(0, BLOCKS, payload, (none, none))
    pay_ref[BLOCKS] = jnp.zeros((8, LANES), F32)
    home_ref[...] = jnp.where(row8 == 0, first, second)
    copy = pltpu.make_async_copy(home_ref, homes_ref, sem)
    copy.start()
    copy.wait()

    def put(i, carry):
        for u in range(4):
            d = i * 4 + u
            first = jnp.clip(homes_ref[0, d], 0, BLOCKS)
            second = jnp.clip(homes_ref[1, d], 0, BLOCKS)
            out_ref[d] = jnp.where(row8 < 4, pay_ref[first], pay_ref[second])
        return carry

    lax.fori_loop(0, BRICKS // 4, put, 0)


def pack_gauss(gcount_ref, mean_ref, opacity_ref, gauss_ref):
    lane = iota((1, LANES), 1)
    for y in range(CY):
        for q in range(QUADS):
            mean = jnp.concatenate([mean_ref[0, y, 4 * q + r] for r in range(4)], axis=1)
            opacity = jnp.concatenate(
                [opacity_ref[0, y, 4 * q + r : 4 * q + r + 1, :] for r in range(4)], axis=1
            )
            have = [gcount_ref[0, y, 4 * q + r] for r in range(4)]
            count = jnp.where(
                lane < 64,
                jnp.where(lane < 32, have[0], have[1]),
                jnp.where(lane < 96, have[2], have[3]),
            )
            opacity = jnp.where((lane & 31) < count, opacity, 0.0)
            gauss_ref[y, q] = jnp.concatenate([mean, opacity, jnp.zeros((4, LANES), F32)], axis=0)


def side(o, last):
    if o == 0:
        return 0, 1, last + 1
    return (last, 0, 1) if o > 0 else (0, last + 2, 1)


def halo_copies(gauss_ref, halo_ref, send_sem, recv_sem):
    copies = []
    for d, (ox, oy, oz) in enumerate(OFFSETS):
        sy, ty, ny = side(oy, CY - 1)
        sq, tq, nq = side(oz, QUADS - 1)
        copies.append(
            pltpu.make_async_remote_copy(
                src_ref=gauss_ref.at[pl.ds(sy, ny), pl.ds(sq, nq)],
                dst_ref=halo_ref.at[1 - ox, pl.ds(ty, ny), pl.ds(tq, nq)],
                send_sem=send_sem.at[d],
                recv_sem=recv_sem.at[d],
                device_id=neighbour((ox, oy, oz)),
                device_id_type=MESH,
            )
        )
    return copies


def near_copies(part_ref, box_ref, send_sem, recv_sem):
    copies = []
    for d, (ox, oy, oz) in enumerate(OFFSETS):
        y0, ny = (1, CY) if oy == 0 else ((CY + 1, 1) if oy > 0 else (0, 1))
        copies.append(
            pltpu.make_async_remote_copy(
                src_ref=part_ref.at[pl.ds((1 + ox) * ROWS + y0, ny)],
                dst_ref=box_ref.at[d, pl.ds(0, ny)],
                send_sem=send_sem.at[d],
                recv_sem=recv_sem.at[d],
                device_id=neighbour((ox, oy, oz)),
                device_id_type=MESH,
            )
        )
    return copies


def inverse_copies(inv_ref, send_sem, recv_sem):
    copies = []
    for d, (ox, oy, oz) in enumerate(OFFSETS):
        sy, ty, ny = side(oy, CY - 1)
        copies.append(
            pltpu.make_async_remote_copy(
                src_ref=inv_ref.at[1, pl.ds(ROWS + 1 + sy, ny)],
                dst_ref=inv_ref.at[1 - oz, pl.ds((1 - ox) * ROWS + ty, ny)],
                send_sem=send_sem.at[d],
                recv_sem=recv_sem.at[d],
                device_id=neighbour((ox, oy, oz)),
                device_id_type=MESH,
            )
        )
    return copies


def feature_windows(halo_ref, win_ref, origin, scale):
    gx, gy, gz = here()
    row8 = iota((8, LANES), 0)
    lane8 = iota((8, LANES), 1)

    def windows(xy, carry):
        x = xy // ROWS
        y = xy % ROWS
        outside = ((x == 0) & (gx == 0)) | ((x == 2) & (gx == SX - 1))
        outside = outside | ((y == 0) & (gy == 0)) | ((y == CY + 1) & (gy == SY - 1))
        tiles = []
        for q in range(QUADS + 2):
            gone = outside
            if q == 0:
                gone = gone | (gz == 0)
            if q == QUADS + 1:
                gone = gone | (gz == SZ - 1)
            tile = halo_ref[x, y, q]
            opacity = jnp.where(gone, 0.0, tile)
            strength = jnp.where(opacity > 0.0, jnp.log2(jnp.maximum(opacity, 1e-30)) - SHARP, GONE)
            tiles.append(jnp.where(row8 == 3, strength, (tile - origin) * scale))
        for z in range(CZ):
            a, b = z // 4, z % 4
            if b == 0:
                tile = pltpu.roll(jnp.where(lane8 >= 96, tiles[a], tiles[a + 1]), 32, 1)
            elif b == 1:
                tile = tiles[a + 1]
            elif b == 2:
                tile = pltpu.roll(tiles[a + 1], 96, 1)
            else:
                tile = pltpu.roll(jnp.where(lane8 < 64, tiles[a + 2], tiles[a + 1]), 64, 1)
            tile = jnp.where((row8 == 3) & (lane8 >= 96), GONE, tile)
            win_ref[z, xy] = jnp.where(row8 == 2, tile - z * SCALE, tile)
        return carry

    lax.fori_loop(0, COLUMNS, windows, 0)


def inverse_windows(inv_ref, win_ref):
    row8 = iota((8, LANES), 0)
    lane1 = iota((1, LANES), 1)

    def windows(xy, carry):
        own = inv_ref[1, xy]
        rows = [inv_ref[0, xy][QUADS - 1 : QUADS]] + [own[q : q + 1] for q in range(QUADS)]
        tile = jnp.concatenate(rows + [inv_ref[2, xy][0:1], jnp.zeros((2, LANES), F32)], axis=0)
        moved = [pltpu.roll(tile, 32, 1), tile, pltpu.roll(tile, 96, 1), pltpu.roll(tile, 64, 1)]
        for z in range(CZ):
            a, b = z // 4, z % 4
            row = moved[b][a + 1 : a + 2]
            if b == 0:
                row = jnp.where(lane1 < 32, moved[b][a : a + 1], row)
            elif b == 3:
                row = jnp.where(lane1 >= 64, moved[b][a + 2 : a + 3], row)
            win_ref[z, xy] = jnp.where(row8 == 4, row, win_ref[z, xy])
        return carry

    lax.fori_loop(0, COLUMNS, windows, 0)


TRIPLES = [(x, dy, divmod(3 * (3 * x + dy), 4)) for x in range(3) for dy in range(3)]


def compose(win_ref, tile_ref):
    lane8 = iota((8, LANES), 1)

    def one(c, carry):
        y = c // CZ
        z = c % CZ
        tiles = [None] * (TILES + 1)
        for x, dy, (j, p) in TRIPLES:
            piece = win_ref[z, x * ROWS + y + dy]
            if p:
                piece = pltpu.roll(piece, 32 * p, 1)
                tiles[j] = jnp.where(lane8 < 32 * p, tiles[j], piece)
            else:
                tiles[j] = piece
            tiles[j + 1] = piece
        for j in range(TILES):
            tile_ref[c, j] = tiles[j]
        return carry

    lax.fori_loop(0, CELLS, one, 0)


def uncompose(acc_ref, wide_ref, count):
    row8 = iota((8, LANES), 0)
    lane8 = iota((8, LANES), 1)
    wide_ref[...] = jnp.zeros_like(wide_ref)

    def one(c, carry):
        y = c // CZ
        z = c % CZ
        tiles = []
        for j in range(TILES):
            rows = [jnp.sum(acc_ref[c, j * count + k], axis=0, keepdims=True) for k in range(count)]
            tile = spread(rows[0])
            for k in range(1, count):
                tile = jnp.where((row8 & 3) == k, rows[k], tile)
            tiles.append(tile)
        for x, dy, (j, p) in TRIPLES:
            tile = tiles[j]
            if p:
                tile = pltpu.roll(jnp.where(lane8 >= 32 * p, tiles[j], tiles[j + 1]), LANES - 32 * p, 1)
            at = x * ROWS + y + dy
            wide_ref[z, at] = wide_ref[z, at] + jnp.where(lane8 < 96, tile, 0.0)
        return carry

    lax.fori_loop(0, CELLS, one, 0)


def fold_quads(wide_ref, xy, lane8):
    quads = [jnp.zeros((8, LANES), F32) for q in range(QUADS + 2)]
    for z in range(CZ):
        tile = wide_ref[z, xy]
        a, b = z // 4, z % 4
        if b == 1:
            quads[a + 1] = quads[a + 1] + tile
        elif b == 2:
            quads[a + 1] = quads[a + 1] + pltpu.roll(tile, 32, 1)
        elif b == 0:
            moved = pltpu.roll(tile, 96, 1)
            quads[a] = quads[a] + jnp.where(lane8 >= 96, moved, 0.0)
            quads[a + 1] = quads[a + 1] + jnp.where(lane8 < 96, moved, 0.0)
        else:
            moved = pltpu.roll(tile, 64, 1)
            quads[a + 1] = quads[a + 1] + jnp.where(lane8 >= 64, moved, 0.0)
            quads[a + 2] = quads[a + 2] + jnp.where(lane8 < 64, moved, 0.0)
    return quads


def decode(in_ref, meta_ref, metas_ref, sem):
    gx, gy, gz = here()
    row8 = iota((8, LANES), 0)
    lane8 = iota((8, LANES), 1)

    def gather(i, found):
        for u in range(32):
            s = i * 32 + u
            found = jnp.where(lane8 == s, jnp.broadcast_to(in_ref[s][:, 0:1], (8, LANES)), found)
        return found

    found = lax.fori_loop(0, BRICKS // 32, gather, jnp.zeros((8, LANES), F32))
    cell = iota((CELLS, LANES), 0).astype(F32)
    lane64 = iota((CELLS, LANES), 1).astype(F32)
    slot = jnp.full((CELLS, LANES), -1.0, F32)
    labels = []
    for k in range(2):
        y0 = jnp.floor(found[4 * k + 1 : 4 * k + 2]) - (gy * CY).astype(F32)
        z0 = jnp.floor(found[4 * k + 2 : 4 * k + 3]) - (gz * CZ).astype(F32)
        label = jnp.where(found[4 * k + 3 : 4 * k + 4] > 0.0, y0 * CZ + z0, -1.0)
        slot = jnp.where(label == cell, 2.0 * lane64 + k, slot)
        labels.append(jnp.clip(label, 0.0, CELLS - 1.0))
    slot = jnp.max(slot, axis=1, keepdims=True)
    meta_ref[pl.ds(0, CELLS), :] = jnp.broadcast_to(slot, (CELLS, LANES)).astype(I32)
    meta_ref[pl.ds(CELLS, 8), :] = jnp.where(row8 == 0, labels[0], labels[1]).astype(I32)
    copy = pltpu.make_async_copy(meta_ref, metas_ref, sem)
    copy.start()
    copy.wait()


def take_points(in_ref, metas_ref, turn_ref, origin, scale):
    row8 = iota((8, LANES), 0)

    def prepare(i, carry):
        for u in range(4):
            c = i * 4 + u
            slot = metas_ref[c, 0]
            safe = jnp.clip(slot, 0, 2 * BRICKS - 1)
            tile = in_ref[safe >> 1]
            tile = jnp.where((safe & 1) == 1, pltpu.roll(tile, 4, 0), tile)
            tile = jnp.where(slot >= 0, tile, 0.0)
            shift = origin + jnp.where(row8 == 2, (c % CZ).astype(F32), 0.0)
            weight = jnp.where(tile > 0.0, jnp.log2(jnp.maximum(tile, 1e-30)), GONE)
            turn_ref[c] = jnp.transpose(jnp.where(row8 == 3, weight, (tile - shift) * scale))
        return carry

    lax.fori_loop(0, CELLS // 4, prepare, 0)


def rows_of(i):
    return i // CHUNKS, i % CHUNKS * (8 * GROUPS)


def broadcasts(turn_ref, i):
    c, first = rows_of(i)
    cols = [turn_ref[c, pl.ds(pl.multiple_of(first + 8 * g, 8), 8), :] for g in range(GROUPS)]
    return [[jnp.broadcast_to(col[:, f : f + 1], (8, LANES)) for f in range(4)] for col in cols]


def keep_features(ahead_ref, feats):
    for g in range(GROUPS):
        for f in range(4):
            ahead_ref[4 * g + f] = feats[g][f]


def first_pass(turn_ref, tile_ref, ahead_ref, late_ref, zp_ref, acc_ref):
    acc_ref[:, 0:TILES] = jnp.zeros((CELLS, TILES, 8, LANES), F32)
    keep_features(ahead_ref, broadcasts(turn_ref, 0))
    for g in range(GROUPS):
        late_ref[g] = jnp.zeros((8, LANES), F32)

    def settle(i):
        for g in range(GROUPS):
            total = jnp.sum(late_ref[g], axis=1, keepdims=True)
            zp_ref[i * GROUPS + g] = jnp.broadcast_to(total, (8, LANES))

    def sweep(i, carry):
        feats = [[ahead_ref[4 * g + f] for f in range(4)] for g in range(GROUPS)]
        settle((i + ITEMS - 1) % ITEMS)
        following = broadcasts(turn_ref, jnp.minimum(i + 1, ITEMS - 1))
        c, first = rows_of(i)
        sums = [None] * GROUPS
        for j in range(TILES):
            mx, my, mz, la = [spread(tile_ref[c, j, f : f + 1, :]) for f in range(4)]
            far = None
            for g in range(GROUPS):
                px, py, pz, lw = feats[g]
                ex, ey, ez = px - mx, py - my, pz - mz
                fall = jnp.exp2(LIFT - ex * ex - ey * ey - ez * ez)
                term = jnp.exp2(fall + (la + lw))
                sums[g] = term if sums[g] is None else sums[g] + term
                far = term if far is None else far + term
            acc_ref[c, j] = acc_ref[c, j] + far
        for g in range(GROUPS):
            late_ref[g] = sums[g]
        keep_features(ahead_ref, following)
        return carry

    lax.fori_loop(0, ITEMS, sweep, 0)
    settle(ITEMS - 1)


def second_pass(turn_ref, tile_ref, ahead_ref, late_ref, zp_ref, acc_ref, stage_ref):
    acc_ref[...] = jnp.zeros_like(acc_ref)
    keep_features(ahead_ref, broadcasts(turn_ref, 0))
    for g in range(4 * GROUPS):
        late_ref[g] = jnp.ones((8, LANES), F32)
    lane = iota((8, LANES), 1) & 3

    def settle(i):
        c, first = rows_of(i)
        for g in range(GROUPS):
            out = (WIDTH * jnp.log(late_ref[4 * g + 3]))
            for k in range(3):
                total = jnp.sum(late_ref[4 * g + k], axis=1, keepdims=True) * BACK
                out = jnp.where(lane == k + 1, total, out)
            stage_ref[c, pl.ds(pl.multiple_of(first + 8 * g, 8), 8), :] = out[:, 0:8]

    def sweep(i, carry):
        feats = [[ahead_ref[4 * g + f] for f in range(4)] for g in range(GROUPS)]
        settle((i + ITEMS - 1) % ITEMS)
        following = broadcasts(turn_ref, jnp.minimum(i + 1, ITEMS - 1))
        c, first = rows_of(i)
        inverse = []
        for g in range(GROUPS):
            lw = feats[g][3]
            total = FLOOR + zp_ref[i * GROUPS + g] * jnp.exp2(-jnp.maximum(lw, -64.0))
            inverse.append(jnp.where(lw > 0.5 * GONE, 1.0 / total, 1.0))
        sums = [[None] * 3 for g in range(GROUPS)]
        for j in range(TILES):
            mx, my, mz, la, ig = [spread(tile_ref[c, j, f : f + 1, :]) for f in range(5)]
            far = [None] * 4
            for g in range(GROUPS):
                px, py, pz, lw = feats[g]
                ex, ey, ez = px - mx, py - my, pz - mz
                fall = jnp.exp2(LIFT - ex * ex - ey * ey - ez * ez)
                term = jnp.exp2(fall + (la + lw))
                pull = (term * fall) * (inverse[g] + ig)
                parts = [pull * ex, pull * ey, pull * ez, term * inverse[g]]
                sums[g] = [p if s is None else s + p for s, p in zip(sums[g], parts)]
                far = [p if s is None else s + p for s, p in zip(far, parts)]
            for k in range(4):
                acc_ref[c, 4 * j + k] = acc_ref[c, 4 * j + k] + far[k]
        for g in range(GROUPS):
            for k in range(3):
                late_ref[4 * g + k] = sums[g][k]
            late_ref[4 * g + 3] = inverse[g]
        keep_features(ahead_ref, following)
        return carry

    lax.fori_loop(0, ITEMS, sweep, 0)
    settle(ITEMS - 1)


def answer_points(stage_ref, res_ref, metas_ref, reply_ref):
    row8 = iota((8, LANES), 0)

    def turn(i, carry):
        for u in range(4):
            res_ref[i * 4 + u] = jnp.transpose(stage_ref[i * 4 + u])
        return carry

    lax.fori_loop(0, CELLS // 4, turn, 0)

    def put(i, carry):
        for u in range(4):
            s = i * 4 + u
            first = jnp.clip(metas_ref[CELLS, s], 0, CELLS - 1)
            second = jnp.clip(metas_ref[CELLS + 1, s], 0, CELLS - 1)
            reply_ref[s] = jnp.where(row8 < 4, res_ref[first], res_ref[second])
        return carry

    lax.fori_loop(0, BRICKS // 4, put, 0)


def quads_of(tile, oz):
    if oz == 0:
        return tile[1 : QUADS + 1]
    row = iota((QUADS, LANES), 0)
    if oz > 0:
        return jnp.where(row == 0, tile[QUADS + 1 : QUADS + 2], 0.0)
    return jnp.where(row == QUADS - 1, tile[0:1], 0.0)


def owner_row(oy, k):
    return k if oy == 0 else (0 if oy > 0 else CY - 1)


def kernel(cell_ref, count_ref, gcount_ref, xyz_ref, weight_ref, mean_ref, opacity_ref,
           point_ref, grad_ref,
           pay_ref, out_ref, in_ref, home_ref, homes_ref, gauss_ref, halo_ref, win_ref, tile_ref,
           meta_ref, metas_ref, turn_ref, ahead_ref, late_ref, zp_ref, acc_ref, wide_ref, part_ref,
           box_ref, inv_ref, loss_ref, stage_ref, res_ref, reply_ref, ans_ref, pull_ref, pulls_ref,
           local_sem, asend, arecv, bsend, brecv, near_sem):
    gx, gy, gz = here()
    me = (gx * SY + gy) * SZ + gz
    row8 = iota((8, LANES), 0)
    lane8 = iota((8, LANES), 1)
    signal_all()
    pack_gauss(gcount_ref, mean_ref, opacity_ref, gauss_ref)
    pack_points(cell_ref, count_ref, xyz_ref, weight_ref, pay_ref, out_ref, home_ref, homes_ref, local_sem.at[0])
    pl.semaphore_wait(pltpu.get_barrier_semaphore(), BRICKS - 1)
    halo = halo_copies(gauss_ref, halo_ref, near_sem.at[0], near_sem.at[1])
    for copy in halo:
        copy.start()
    exchange_start(out_ref, in_ref, asend, arecv)
    in_ref[me] = out_ref[me]
    for y in range(CY):
        for q in range(QUADS):
            halo_ref[1, y + 1, q + 1] = gauss_ref[y, q]
    origin = jnp.where(row8 == 0, gx, jnp.where(row8 == 1, gy * CY + CY // 2, gz * CZ)).astype(F32)
    origin = jnp.where(row8 < 3, origin, 0.0)
    scale = jnp.where(row8 < 3, SCALE, 1.0).astype(F32)
    for copy in halo:
        copy.wait()
    feature_windows(halo_ref, win_ref, origin, scale)
    compose(win_ref, tile_ref)
    exchange_wait(out_ref, in_ref, asend, arecv)
    decode(in_ref, meta_ref, metas_ref, local_sem.at[1])
    take_points(in_ref, metas_ref, turn_ref, origin, scale)

    first_pass(turn_ref, tile_ref, ahead_ref, late_ref, zp_ref, acc_ref)
    uncompose(acc_ref, wide_ref, 1)

    def fold(xy, carry):
        quads = fold_quads(wide_ref, xy, lane8)
        part_ref[xy] = jnp.concatenate([quad[0:1] for quad in quads] + [jnp.zeros((2, LANES), F32)], axis=0)
        return carry

    lax.fori_loop(0, COLUMNS, fold, 0)
    copies = near_copies(part_ref, box_ref, near_sem.at[2], near_sem.at[3])
    for copy in copies:
        copy.start()
    sums = [part_ref[ROWS + y + 1][1 : QUADS + 1] for y in range(CY)]
    for d, (ox, oy, oz) in enumerate(OFFSETS):
        copies[d].wait_recv()
        for k in range(CY if oy == 0 else 1):
            y = owner_row(oy, k)
            sums[y] = sums[y] + quads_of(box_ref[d, k], oz)
    for y in range(CY):
        opacity = jnp.concatenate([gauss_ref[y, q][3:4] for q in range(QUADS)], axis=0)
        valid = opacity > 0.0
        total_g = FLOOR + jnp.where(valid, sums[y] / jnp.where(valid, opacity, 1.0), 0.0)
        blank = jnp.zeros((8 - QUADS, LANES), F32)
        inv_ref[1, ROWS + y + 1] = jnp.concatenate([1.0 / total_g, blank], axis=0)
        loss = jnp.where(valid, -WIDTH * jnp.log(total_g), 0.0)
        loss_ref[y] = jnp.concatenate([loss, opacity], axis=0)
    back = inverse_copies(inv_ref, near_sem.at[4], near_sem.at[5])
    for copy in back:
        copy.start()
    for copy in copies:
        copy.wait_send()
    for copy in back:
        copy.wait()
    inverse_windows(inv_ref, win_ref)
    compose(win_ref, tile_ref)

    second_pass(turn_ref, tile_ref, ahead_ref, late_ref, zp_ref, acc_ref, stage_ref)
    answer_points(stage_ref, res_ref, metas_ref, reply_ref)
    exchange_start(reply_ref, ans_ref, bsend, brecv)
    ans_ref[me] = reply_ref[me]
    uncompose(acc_ref, wide_ref, 4)

    def fold_pull(xy, carry):
        quads = fold_quads(wide_ref, xy, lane8)
        for m in range(3):
            pull_ref[xy, m] = jnp.where(row8 < 4, quads[2 * m], quads[2 * m + 1])
        return carry

    lax.fori_loop(0, COLUMNS, fold_pull, 0)
    copies = near_copies(pull_ref, pulls_ref, near_sem.at[6], near_sem.at[7])
    for copy in copies:
        copy.start()
    sums = [[pull_ref[ROWS + y + 1, m] for m in range(3)] for y in range(CY)]
    for d, (ox, oy, oz) in enumerate(OFFSETS):
        copies[d].wait_recv()
        for k in range(CY if oy == 0 else 1):
            y = owner_row(oy, k)
            if oz == 0:
                for m in range(3):
                    sums[y][m] = sums[y][m] + pulls_ref[d, k, m]
            elif oz > 0:
                sums[y][0] = sums[y][0] + jnp.where(row8 >= 4, pulls_ref[d, k, 2], 0.0)
            else:
                sums[y][2] = sums[y][2] + jnp.where(row8 < 4, pulls_ref[d, k, 0], 0.0)
    for y in range(CY):
        for q in range(QUADS):
            m, half = divmod(q + 1, 2)
            tile = sums[y][m][4 * half : 4 * half + 4]
            loss = loss_ref[y][q : q + 1]
            opacity = loss_ref[y][QUADS + q : QUADS + q + 1]
            valid = opacity > 0.0
            dense = loss - WIDTH * (tile / jnp.where(valid, opacity, 1.0))
            tile = jnp.where(iota((4, LANES), 0) < 3, tile * (-BACK), dense)
            tile = jnp.where(valid, tile, 0.0)
            for r in range(4):
                grad_ref[0, y, 4 * q + r] = tile[:, SLOTS * r : SLOTS * r + SLOTS]
    for copy in copies:
        copy.wait_send()
    exchange_wait(reply_ref, ans_ref, bsend, brecv)

    def place(b, carry):
        cell = cell_ref[b]
        brick = ((cell >> 10 & 7) * SY + (cell >> 8 & 3)) * SZ + (cell >> 4 & 3)
        tile = ans_ref[brick]
        tile = jnp.where(homes_ref[0, brick] == b, tile, pltpu.roll(tile, 4, 0))
        point_ref[b] = tile[0:4]
        return carry

    lax.fori_loop(0, BLOCKS, place, 0)


def on_device(point_xyz, point_weight, block_cell, block_count, gauss_mean, gauss_opacity, gauss_count):
    dma = pltpu.SemaphoreType.DMA
    return pl.pallas_call(
        kernel,
        out_shape=(
            jax.ShapeDtypeStruct((BLOCKS, 4, LANES), F32),
            jax.ShapeDtypeStruct((1, CY, CZ, 4, SLOTS), F32),
        ),
        in_specs=[SMEM, SMEM, SMEM, VMEM, VMEM, VMEM, VMEM],
        out_specs=(VMEM, VMEM),
        scratch_shapes=[
            pltpu.VMEM((BLOCKS + 1, 8, LANES), F32),
            pltpu.VMEM((BRICKS, 8, LANES), F32),
            pltpu.VMEM((BRICKS, 8, LANES), F32),
            pltpu.VMEM((8, LANES), I32),
            pltpu.SMEM((8, LANES), I32),
            pltpu.VMEM((CY, QUADS, 8, LANES), F32),
            pltpu.VMEM((3, ROWS, QUADS + 2, 8, LANES), F32),
            pltpu.VMEM((CZ, COLUMNS, 8, LANES), F32),
            pltpu.VMEM((CELLS, TILES, 8, LANES), F32),
            pltpu.VMEM((CELLS + 8, LANES), I32),
            pltpu.SMEM((CELLS + 8, LANES), I32),
            pltpu.VMEM((CELLS, LANES, 8), F32),
            pltpu.VMEM((4 * GROUPS, 8, LANES), F32),
            pltpu.VMEM((4 * GROUPS, 8, LANES), F32),
            pltpu.VMEM((ITEMS * GROUPS, 8, LANES), F32),
            pltpu.VMEM((CELLS, 4 * TILES, 8, LANES), F32),
            pltpu.VMEM((CZ, COLUMNS, 8, LANES), F32),
            pltpu.VMEM((COLUMNS, 8, LANES), F32),
            pltpu.VMEM((26, CY, 8, LANES), F32),
            pltpu.VMEM((3, COLUMNS, 8, LANES), F32),
            pltpu.VMEM((CY, 8, LANES), F32),
            pltpu.VMEM((CELLS, LANES, 8), F32),
            pltpu.VMEM((CELLS, 8, LANES), F32),
            pltpu.VMEM((BRICKS, 8, LANES), F32),
            pltpu.VMEM((BRICKS, 8, LANES), F32),
            pltpu.VMEM((COLUMNS, 3, 8, LANES), F32),
            pltpu.VMEM((26, CY, 3, 8, LANES), F32),
            dma((2,)),
            dma((BRICKS,)),
            dma((BRICKS,)),
            dma((BRICKS,)),
            dma((BRICKS,)),
            dma((8, 26)),
        ],
        compiler_params=pltpu.CompilerParams(
            collective_id=0, has_side_effects=True, vmem_limit_bytes=56 * 1024 * 1024
        ),
        name="chamfer",
    )(block_cell, block_count, gauss_count, point_xyz, point_weight, gauss_mean, gauss_opacity)


def solution(mesh):
    return jax.shard_map(
        on_device,
        mesh=mesh,
        in_specs=(
            P(AXES, None, None),
            P(AXES, None),
            P(AXES),
            P(AXES),
            P("gx", "gy", "gz", None, None),
            P("gx", "gy", "gz", None),
            P("gx", "gy", "gz"),
        ),
        out_specs=(P(AXES, None, None), P("gx", "gy", "gz", None, None)),
        check_vma=False,
    )
```

time: 341 us -> 189 us (0.55)
  Pallas kernels: 0 us -> 184 us
  other arithmetic: 145 us -> 0 us
  starting transfers between devices: 96.6 us -> 0 us
  waiting for transfers between devices: 55.9 us -> 0 us
  local copies, waits for them, and re-layouts: 32.7 us -> 4.54 us
  loops' own time: 8.24 us -> 0 us
    pallas_call x0 -> x1, Pallas kernels: none -> 184 us  [on_device(): pl.pallas_call(kernel, out_shape=(jax.ShapeDtypeStruct((BLOCKS, 4, LANES)...]
    reduce_sum x55 -> x0, other arithmetic: 132 us -> none  [the longest x27 82.2 us: pair_block(): jnp.sum(coupling * delta_x, axis=-2)]
    ppermute x24 -> x0, starting transfers between devices: 65.8 us -> none  [the longest x12 47 us: with_halo(): lax.ppermute(tail, axis, [(i, (i + 1) % count) for i in range(ends)])]
    ppermute x24 -> x0, waiting for transfers between devices: 40.6 us -> none  [the longest x12 32.6 us: with_halo(): lax.ppermute(head, axis, [((i + 1) % count, i) for i in range(ends)])]
    all_to_all x3 -> x0, starting transfers between devices: 30.8 us -> none  [the longest x1 11.5 us: on_device(): lax.all_to_all(labels, ('gx', 'gy', 'gz'), split_axis=0, concat_axis=0, t...]
    all_to_all x3 -> x0, waiting for transfers between devices: 15.3 us -> none  [the longest x1 12.4 us: on_device(): lax.all_to_all(reply_rows, ('gx', 'gy', 'gz'), split_axis=0, concat_axis=...]
    scatter x3 -> x0, local copies, waits for them, and re-layouts: 13.4 us -> none  [the longest x1 7.62 us: on_device(): jnp.zeros((cell_total, 4, points_len), jnp.float32).at[placed]]
    dynamic_update_slice x54 -> x0, local copies, waits for them, and re-layouts: 11 us -> none  [put_window(): return lax.dynamic_update_slice(values, update, corner)]
  transfers between devices with their start and end apart: 27 -> 0, of which waited for: 14 -> 0; matrix products, arithmetic and copies ran while one was open for 5% -> 0% of each run, Pallas kernels for 0% -> 0%
where the time goes in v2:
time: 189 us
  Pallas kernels  184 us (97%)
  local copies, waits for them, and re-layouts  4.54 us (2%)
    pallas_call x1, Pallas kernels, on_device(): pl.pallas_call(kernel, out_shape=(jax.ShapeDtypeStruct((BLOCKS, 4, LANES)...  184 us
    unnamed x8, local copies, waits for them, and re-layouts  4.54 us

profile of v2, /device:TPU:1, one launch (start us, length us, event | category | flops | bytes accessed | tf_op | source)
XLA Modules:
  0.0 188.7 jit_solution(12373408220156188397)
XLA Ops:
  0.6 0.0 copy-start.1
  0.6 1.6 copy.9.xyz_ref
  2.2 0.0 copy-done.1
  2.2 0.7 copy.10.mean_ref
  2.9 183.5 %chamfer.1 = (f32[48,4,128]{2,1,0:T(4,128)}, f32[1,4,16,4,32]{4,3,2,1,0:T(4,128)}) custom-call(s32[48]{0:T(128)} %cell_ref.1, s32[48]{0:T(128)} %count_ref.1, s32[1,4,16]{2,1,0:T(4,128)} %gcount_ref.1, f32[48,3,128]{2,1,0:T(4,128)} %copy.9.xyz_ref, f32[48,128]{1,0:T(8,128)} %weight_ref.1, f32[1,4,16,3,32]{4,3,2,1,0:T(4,128)} %copy.10.mean_ref, ...), custom_call_target="tpu_custom_call" | custom-call | tf_op jit(solution)/shard_map/chamfer/pallas_call | solution.py:684
  186.5 0.0 copy-start
  186.5 1.6 copy.13
  188.0 0.0 copy-done
  188.0 0.7 copy.14
Async XLA Ops:
  0.6 1.6 copy-start.1
  186.5 1.6 copy-start

commit v3 on v2

--- a/solution.py
+++ b/solution.py
@@ -17,9 +17,8 @@
 SLOTS = 32
 LANES = 128
 QUADS = CZ // 4
-GROUPS = 4
-CHUNKS = LANES // (8 * GROUPS)
-ITEMS = CELLS * CHUNKS
+FIRST_GROUPS = 8
+SECOND_GROUPS = 4
 TILES = 7
 ROWS = CY + 2
 COLUMNS = 3 * ROWS
@@ -70,34 +69,43 @@
     return ((gx + ox + SX) % SX, (gy + oy + SY) % SY, (gz + oz + SZ) % SZ)
 
 
-def exchange_copy(src_ref, dst_ref, send_sem, recv_sem, i):
+def every_peer(act):
+    gx, gy, gz = here()
+    near = [((gy + dy) % SY, (gz + dz) % SZ) for dy in range(SY) for dz in range(SZ)]
+
+    def plane(dx, first):
+        px = (gx + dx) % SX
+        for k in range(first, SY * SZ):
+            py, pz = near[k]
+            act(dx * (SY * SZ) + k, px * (SY * SZ) + (py * SZ + pz), (px, py, pz))
+
+    def step(dx, carry):
+        plane(dx, 0)
+        return carry
+
+    lax.fori_loop(1, SX, step, 0)
+    plane(0, 1)
+
+
+def exchange_copy(src_ref, dst_ref, send_sem, recv_sem, i, peer, device):
     gx, gy, gz = here()
     me = (gx * SY + gy) * SZ + gz
-    peer = (me + i) % BRICKS
     return pltpu.make_async_remote_copy(
         src_ref=src_ref.at[peer],
         dst_ref=dst_ref.at[me],
         send_sem=send_sem.at[i],
         recv_sem=recv_sem.at[i],
-        device_id=place_of(peer),
+        device_id=device,
         device_id_type=MESH,
     )
 
 
 def exchange_start(*refs):
-    def step(i, carry):
-        exchange_copy(*refs, i).start()
-        return carry
-
-    lax.fori_loop(1, BRICKS, step, 0)
+    every_peer(lambda i, peer, device: exchange_copy(*refs, i, peer, device).start())
 
 
 def exchange_wait(*refs):
-    def step(i, carry):
-        exchange_copy(*refs, i).wait()
-        return carry
-
-    lax.fori_loop(1, BRICKS, step, 0)
+    every_peer(lambda i, peer, device: exchange_copy(*refs, i, peer, device).wait())
 
 
 def spread(row):
@@ -105,15 +113,10 @@
 
 
 def signal_all():
-    gx, gy, gz = here()
-    me = (gx * SY + gy) * SZ + gz
     barrier = pltpu.get_barrier_semaphore()
-
-    def signal(i, carry):
-        pl.semaphore_signal(barrier, inc=1, device_id=place_of((me + i) % BRICKS), device_id_type=MESH)
-        return carry
-
-    lax.fori_loop(1, BRICKS, signal, 0)
+    every_peer(
+        lambda i, peer, device: pl.semaphore_signal(barrier, inc=1, device_id=device, device_id_type=MESH)
+    )
 
 
 def pack_points(cell_ref, count_ref, xyz_ref, weight_ref, pay_ref, out_ref, home_ref, homes_ref, sem):
@@ -134,7 +137,7 @@
         second = jnp.where(later, b, second)
         first = jnp.where(hit & (first == BLOCKS), b, first)
         weight = jnp.where(lane < count_ref[b], weight_ref[pl.ds(b, 1), :], 0.0)
-        rows = jnp.concatenate([xyz_ref[b], weight], axis=0)
+        rows = jnp.concatenate([xyz_ref[k, pl.ds(b, 1), :] for k in range(3)] + [weight], axis=0)
         corner = jnp.where(row4 == 0, cx, jnp.where(row4 == 1, cy, cz))
         top = (corner + 1).astype(F32) - NUDGE
         rows = jnp.where((lane4 == 0) & (row4 < 3), jnp.minimum(rows, top), rows)
@@ -164,7 +167,7 @@
     lane = iota((1, LANES), 1)
     for y in range(CY):
         for q in range(QUADS):
-            mean = jnp.concatenate([mean_ref[0, y, 4 * q + r] for r in range(4)], axis=1)
+            mean = jnp.concatenate([mean_ref[0, y, :, 4 * q + r, :] for r in range(4)], axis=1)
             opacity = jnp.concatenate(
                 [opacity_ref[0, y, 4 * q + r : 4 * q + r + 1, :] for r in range(4)], axis=1
             )
@@ -191,8 +194,8 @@
         sq, tq, nq = side(oz, QUADS - 1)
         copies.append(
             pltpu.make_async_remote_copy(
-                src_ref=gauss_ref.at[pl.ds(sy, ny), pl.ds(sq, nq)],
-                dst_ref=halo_ref.at[1 - ox, pl.ds(ty, ny), pl.ds(tq, nq)],
+                src_ref=gauss_ref.at[pl.ds(sy, ny), pl.ds(sq, nq), pl.ds(0, 4)],
+                dst_ref=halo_ref.at[1 - ox, pl.ds(ty, ny), pl.ds(tq, nq), pl.ds(0, 4)],
                 send_sem=send_sem.at[d],
                 recv_sem=recv_sem.at[d],
                 device_id=neighbour((ox, oy, oz)),
@@ -219,6 +222,24 @@
     return copies
 
 
+def pull_copies(pull_ref, box_ref, send_sem, recv_sem):
+    copies = []
+    for d, (ox, oy, oz) in enumerate(OFFSETS):
+        y0, ny = (1, CY) if oy == 0 else ((CY + 1, 1) if oy > 0 else (0, 1))
+        m0, nm = (0, 2) if oz == 0 else (2, 1)
+        copies.append(
+            pltpu.make_async_remote_copy(
+                src_ref=pull_ref.at[pl.ds(m0, nm), pl.ds((1 + ox) * ROWS + y0, ny)],
+                dst_ref=box_ref.at[d, pl.ds(0, nm), pl.ds(0, ny)],
+                send_sem=send_sem.at[d],
+                recv_sem=recv_sem.at[d],
+                device_id=neighbour((ox, oy, oz)),
+                device_id_type=MESH,
+            )
+        )
+    return copies
+
+
 def inverse_copies(inv_ref, send_sem, recv_sem):
     copies = []
     for d, (ox, oy, oz) in enumerate(OFFSETS):
@@ -241,9 +262,13 @@
     row8 = iota((8, LANES), 0)
     lane8 = iota((8, LANES), 1)
 
-    def windows(xy, carry):
-        x = xy // ROWS
-        y = xy % ROWS
+    def windows(y, carry):
+        for x in range(3):
+            window(x, y)
+        return carry
+
+    def window(x, y):
+        xy = x * ROWS + y
         outside = ((x == 0) & (gx == 0)) | ((x == 2) & (gx == SX - 1))
         outside = outside | ((y == 0) & (gy == 0)) | ((y == CY + 1) & (gy == SY - 1))
         tiles = []
@@ -269,16 +294,20 @@
                 tile = pltpu.roll(jnp.where(lane8 < 64, tiles[a + 2], tiles[a + 1]), 64, 1)
             tile = jnp.where((row8 == 3) & (lane8 >= 96), GONE, tile)
             win_ref[z, xy] = jnp.where(row8 == 2, tile - z * SCALE, tile)
-        return carry
-
-    lax.fori_loop(0, COLUMNS, windows, 0)
+
+    lax.fori_loop(0, ROWS, windows, 0)
 
 
 def inverse_windows(inv_ref, win_ref):
     row8 = iota((8, LANES), 0)
     lane1 = iota((1, LANES), 1)
 
-    def windows(xy, carry):
+    def windows(y, carry):
+        for x in range(3):
+            window(x * ROWS + y)
+        return carry
+
+    def window(xy):
         own = inv_ref[1, xy]
         rows = [inv_ref[0, xy][QUADS - 1 : QUADS]] + [own[q : q + 1] for q in range(QUADS)]
         tile = jnp.concatenate(rows + [inv_ref[2, xy][0:1], jnp.zeros((2, LANES), F32)], axis=0)
@@ -291,9 +320,8 @@
             elif b == 3:
                 row = jnp.where(lane1 >= 64, moved[b][a + 2 : a + 3], row)
             win_ref[z, xy] = jnp.where(row8 == 4, row, win_ref[z, xy])
-        return carry
-
-    lax.fori_loop(0, COLUMNS, windows, 0)
+
+    lax.fori_loop(0, ROWS, windows, 0)
 
 
 TRIPLES = [(x, dy, divmod(3 * (3 * x + dy), 4)) for x in range(3) for dy in range(3)]
@@ -302,46 +330,56 @@
 def compose(win_ref, tile_ref):
     lane8 = iota((8, LANES), 1)
 
-    def one(c, carry):
-        y = c // CZ
-        z = c % CZ
-        tiles = [None] * (TILES + 1)
-        for x, dy, (j, p) in TRIPLES:
-            piece = win_ref[z, x * ROWS + y + dy]
-            if p:
-                piece = pltpu.roll(piece, 32 * p, 1)
-                tiles[j] = jnp.where(lane8 < 32 * p, tiles[j], piece)
-            else:
-                tiles[j] = piece
-            tiles[j + 1] = piece
-        for j in range(TILES):
-            tile_ref[c, j] = tiles[j]
-        return carry
-
-    lax.fori_loop(0, CELLS, one, 0)
+    def one(z, carry):
+        for y in range(CY):
+            tiles = [None] * (TILES + 1)
+            for x, dy, (j, p) in TRIPLES:
+                piece = win_ref[z, x * ROWS + y + dy]
+                if p:
+                    piece = pltpu.roll(piece, 32 * p, 1)
+                    tiles[j] = jnp.where(lane8 < 32 * p, tiles[j], piece)
+                else:
+                    tiles[j] = piece
+                tiles[j + 1] = piece
+            for j in range(TILES):
+                tile_ref[y * CZ + z, j] = tiles[j]
+        return carry
+
+    lax.fori_loop(0, CZ, one, 0)
 
 
 def uncompose(acc_ref, wide_ref, count):
     row8 = iota((8, LANES), 0)
     lane8 = iota((8, LANES), 1)
-    wide_ref[...] = jnp.zeros_like(wide_ref)
-
+
+    def one(z, carry):
+        wide = [None] * COLUMNS
+        for y in range(CY):
+            tiles = []
+            for j in range(TILES):
+                at = y * CZ + z
+                rows = [jnp.sum(acc_ref[at, j * count + k], axis=0, keepdims=True) for k in range(count)]
+                tile = spread(rows[0])
+                for k in range(1, count):
+                    tile = jnp.where((row8 & 3) == k, rows[k], tile)
+                tiles.append(tile)
+            for x, dy, (j, p) in TRIPLES:
+                tile = tiles[j]
+                if p:
+                    tile = pltpu.roll(jnp.where(lane8 >= 32 * p, tiles[j], tiles[j + 1]), LANES - 32 * p, 1)
+                at = x * ROWS + y + dy
+                wide[at] = tile if wide[at] is None else wide[at] + tile
+        for at in range(COLUMNS):
+            wide_ref[z, at] = jnp.where(lane8 < 96, wide[at], 0.0)
+        return carry
+
+    lax.fori_loop(0, CZ, one, 0)
+
+
+def clear(acc_ref):
     def one(c, carry):
-        y = c // CZ
-        z = c % CZ
-        tiles = []
-        for j in range(TILES):
-            rows = [jnp.sum(acc_ref[c, j * count + k], axis=0, keepdims=True) for k in range(count)]
-            tile = spread(rows[0])
-            for k in range(1, count):
-                tile = jnp.where((row8 & 3) == k, rows[k], tile)
-            tiles.append(tile)
-        for x, dy, (j, p) in TRIPLES:
-            tile = tiles[j]
-            if p:
-                tile = pltpu.roll(jnp.where(lane8 >= 32 * p, tiles[j], tiles[j + 1]), LANES - 32 * p, 1)
-            at = x * ROWS + y + dy
-            wide_ref[z, at] = wide_ref[z, at] + jnp.where(lane8 < 96, tile, 0.0)
+        for j in range(4 * TILES):
+            acc_ref[c, j] = jnp.zeros((8, LANES), F32)
         return carry
 
     lax.fori_loop(0, CELLS, one, 0)
@@ -397,12 +435,12 @@
     copy.wait()
 
 
-def take_points(in_ref, metas_ref, turn_ref, origin, scale):
+def take_points(in_ref, metas_ref, pts_ref, origin, scale):
     row8 = iota((8, LANES), 0)
 
     def prepare(i, carry):
-        for u in range(4):
-            c = i * 4 + u
+        for u in range(8):
+            c = i * 8 + u
             slot = metas_ref[c, 0]
             safe = jnp.clip(slot, 0, 2 * BRICKS - 1)
             tile = in_ref[safe >> 1]
@@ -410,49 +448,47 @@
             tile = jnp.where(slot >= 0, tile, 0.0)
             shift = origin + jnp.where(row8 == 2, (c % CZ).astype(F32), 0.0)
             weight = jnp.where(tile > 0.0, jnp.log2(jnp.maximum(tile, 1e-30)), GONE)
-            turn_ref[c] = jnp.transpose(jnp.where(row8 == 3, weight, (tile - shift) * scale))
-        return carry
-
-    lax.fori_loop(0, CELLS // 4, prepare, 0)
-
-
-def rows_of(i):
-    return i // CHUNKS, i % CHUNKS * (8 * GROUPS)
-
-
-def broadcasts(turn_ref, i):
-    c, first = rows_of(i)
-    cols = [turn_ref[c, pl.ds(pl.multiple_of(first + 8 * g, 8), 8), :] for g in range(GROUPS)]
-    return [[jnp.broadcast_to(col[:, f : f + 1], (8, LANES)) for f in range(4)] for col in cols]
-
-
-def keep_features(ahead_ref, feats):
-    for g in range(GROUPS):
-        for f in range(4):
-            ahead_ref[4 * g + f] = feats[g][f]
-
-
-def first_pass(turn_ref, tile_ref, ahead_ref, late_ref, zp_ref, acc_ref):
-    acc_ref[:, 0:TILES] = jnp.zeros((CELLS, TILES, 8, LANES), F32)
-    keep_features(ahead_ref, broadcasts(turn_ref, 0))
-    for g in range(GROUPS):
+            pts_ref[c] = jnp.where(row8 == 3, weight, (tile - shift) * scale)
+        return carry
+
+    lax.fori_loop(0, CELLS // 8, prepare, 0)
+    pts_ref[CELLS] = jnp.zeros((8, LANES), F32)
+
+
+def rows_of(i, groups):
+    chunks = LANES // (8 * groups)
+    return i // chunks, i % chunks * (8 * groups)
+
+
+def turn(pts_ref, feat_ref, c, f):
+    row = jnp.broadcast_to(pts_ref[c, pl.ds(f, 1), :], (LANES, LANES))
+    feat_ref[f, pl.ds(c * 16, 16)] = jnp.transpose(row).reshape(16, 8, LANES)
+
+
+def first_pass(pts_ref, feat_ref, tile_ref, late_ref, zp_ref, acc_ref):
+    groups = FIRST_GROUPS
+    items = CELLS * LANES // (8 * groups)
+    for f in range(4):
+        turn(pts_ref, feat_ref, 0, f)
+    for g in range(groups):
         late_ref[g] = jnp.zeros((8, LANES), F32)
 
     def settle(i):
-        for g in range(GROUPS):
+        for g in range(groups):
             total = jnp.sum(late_ref[g], axis=1, keepdims=True)
-            zp_ref[i * GROUPS + g] = jnp.broadcast_to(total, (8, LANES))
+            zp_ref[i * groups + g] = jnp.broadcast_to(total, (8, LANES))
 
     def sweep(i, carry):
-        feats = [[ahead_ref[4 * g + f] for f in range(4)] for g in range(GROUPS)]
-        settle((i + ITEMS - 1) % ITEMS)
-        following = broadcasts(turn_ref, jnp.minimum(i + 1, ITEMS - 1))
-        c, first = rows_of(i)
-        sums = [None] * GROUPS
+        feats = [[feat_ref[f, i * groups + g] for f in range(4)] for g in range(groups)]
+        settle((i + items - 1) % items)
+        for f in range(2):
+            turn(pts_ref, feat_ref, i // 2 + 1, i % 2 * 2 + f)
+        c, first = rows_of(i, groups)
+        sums = [None] * groups
         for j in range(TILES):
             mx, my, mz, la = [spread(tile_ref[c, j, f : f + 1, :]) for f in range(4)]
             far = None
-            for g in range(GROUPS):
+            for g in range(groups):
                 px, py, pz, lw = feats[g]
                 ex, ey, ez = px - mx, py - my, pz - mz
                 fall = jnp.exp2(LIFT - ex * ex - ey * ey - ez * ez)
@@ -460,25 +496,24 @@
                 sums[g] = term if sums[g] is None else sums[g] + term
                 far = term if far is None else far + term
             acc_ref[c, j] = acc_ref[c, j] + far
-        for g in range(GROUPS):
+        for g in range(groups):
             late_ref[g] = sums[g]
-        keep_features(ahead_ref, following)
-        return carry
-
-    lax.fori_loop(0, ITEMS, sweep, 0)
-    settle(ITEMS - 1)
-
-
-def second_pass(turn_ref, tile_ref, ahead_ref, late_ref, zp_ref, acc_ref, stage_ref):
-    acc_ref[...] = jnp.zeros_like(acc_ref)
-    keep_features(ahead_ref, broadcasts(turn_ref, 0))
-    for g in range(4 * GROUPS):
+        return carry
+
+    lax.fori_loop(0, items, sweep, 0)
+    settle(items - 1)
+
+
+def second_pass(feat_ref, tile_ref, late_ref, zp_ref, acc_ref, stage_ref):
+    groups = SECOND_GROUPS
+    items = CELLS * LANES // (8 * groups)
+    for g in range(4 * groups):
         late_ref[g] = jnp.ones((8, LANES), F32)
     lane = iota((8, LANES), 1) & 3
 
     def settle(i):
-        c, first = rows_of(i)
-        for g in range(GROUPS):
+        c, first = rows_of(i, groups)
+        for g in range(groups):
             out = (WIDTH * jnp.log(late_ref[4 * g + 3]))
             for k in range(3):
                 total = jnp.sum(late_ref[4 * g + k], axis=1, keepdims=True) * BACK
@@ -486,20 +521,19 @@
             stage_ref[c, pl.ds(pl.multiple_of(first + 8 * g, 8), 8), :] = out[:, 0:8]
 
     def sweep(i, carry):
-        feats = [[ahead_ref[4 * g + f] for f in range(4)] for g in range(GROUPS)]
-        settle((i + ITEMS - 1) % ITEMS)
-        following = broadcasts(turn_ref, jnp.minimum(i + 1, ITEMS - 1))
-        c, first = rows_of(i)
+        feats = [[feat_ref[f, i * groups + g] for f in range(4)] for g in range(groups)]
+        settle((i + items - 1) % items)
+        c, first = rows_of(i, groups)
         inverse = []
-        for g in range(GROUPS):
+        for g in range(groups):
             lw = feats[g][3]
-            total = FLOOR + zp_ref[i * GROUPS + g] * jnp.exp2(-jnp.maximum(lw, -64.0))
+            total = FLOOR + zp_ref[i * groups + g] * jnp.exp2(-jnp.maximum(lw, -64.0))
             inverse.append(jnp.where(lw > 0.5 * GONE, 1.0 / total, 1.0))
-        sums = [[None] * 3 for g in range(GROUPS)]
+        sums = [[None] * 3 for g in range(groups)]
         for j in range(TILES):
             mx, my, mz, la, ig = [spread(tile_ref[c, j, f : f + 1, :]) for f in range(5)]
             far = [None] * 4
-            for g in range(GROUPS):
+            for g in range(groups):
                 px, py, pz, lw = feats[g]
                 ex, ey, ez = px - mx, py - my, pz - mz
                 fall = jnp.exp2(LIFT - ex * ex - ey * ey - ez * ez)
@@ -510,26 +544,25 @@
                 far = [p if s is None else s + p for s, p in zip(far, parts)]
             for k in range(4):
                 acc_ref[c, 4 * j + k] = acc_ref[c, 4 * j + k] + far[k]
-        for g in range(GROUPS):
+        for g in range(groups):
             for k in range(3):
                 late_ref[4 * g + k] = sums[g][k]
             late_ref[4 * g + 3] = inverse[g]
-        keep_features(ahead_ref, following)
-        return carry
-
-    lax.fori_loop(0, ITEMS, sweep, 0)
-    settle(ITEMS - 1)
+        return carry
+
+    lax.fori_loop(0, items, sweep, 0)
+    settle(items - 1)
 
 
 def answer_points(stage_ref, res_ref, metas_ref, reply_ref):
     row8 = iota((8, LANES), 0)
 
     def turn(i, carry):
-        for u in range(4):
-            res_ref[i * 4 + u] = jnp.transpose(stage_ref[i * 4 + u])
-        return carry
-
-    lax.fori_loop(0, CELLS // 4, turn, 0)
+        for u in range(8):
+            res_ref[i * 8 + u] = jnp.transpose(stage_ref[i * 8 + u])
+        return carry
+
+    lax.fori_loop(0, CELLS // 8, turn, 0)
 
     def put(i, carry):
         for u in range(4):
@@ -558,7 +591,7 @@
 def kernel(cell_ref, count_ref, gcount_ref, xyz_ref, weight_ref, mean_ref, opacity_ref,
            point_ref, grad_ref,
            pay_ref, out_ref, in_ref, home_ref, homes_ref, gauss_ref, halo_ref, win_ref, tile_ref,
-           meta_ref, metas_ref, turn_ref, ahead_ref, late_ref, zp_ref, acc_ref, wide_ref, part_ref,
+           meta_ref, metas_ref, pts_ref, feat_ref, late_ref, zp_ref, acc_ref, wide_ref, part_ref,
            box_ref, inv_ref, loss_ref, stage_ref, res_ref, reply_ref, ans_ref, pull_ref, pulls_ref,
            local_sem, asend, arecv, bsend, brecv, near_sem):
     gx, gy, gz = here()
@@ -584,22 +617,26 @@
         copy.wait()
     feature_windows(halo_ref, win_ref, origin, scale)
     compose(win_ref, tile_ref)
+    clear(acc_ref)
     exchange_wait(out_ref, in_ref, asend, arecv)
     decode(in_ref, meta_ref, metas_ref, local_sem.at[1])
-    take_points(in_ref, metas_ref, turn_ref, origin, scale)
-
-    first_pass(turn_ref, tile_ref, ahead_ref, late_ref, zp_ref, acc_ref)
+    take_points(in_ref, metas_ref, pts_ref, origin, scale)
+
+    first_pass(pts_ref, feat_ref, tile_ref, late_ref, zp_ref, acc_ref)
     uncompose(acc_ref, wide_ref, 1)
 
-    def fold(xy, carry):
-        quads = fold_quads(wide_ref, xy, lane8)
-        part_ref[xy] = jnp.concatenate([quad[0:1] for quad in quads] + [jnp.zeros((2, LANES), F32)], axis=0)
-        return carry
-
-    lax.fori_loop(0, COLUMNS, fold, 0)
+    def fold(y, carry):
+        for x in range(3):
+            quads = fold_quads(wide_ref, x * ROWS + y, lane8)
+            rows = [quad[0:1] for quad in quads] + [jnp.zeros((2, LANES), F32)]
+            part_ref[x * ROWS + y] = jnp.concatenate(rows, axis=0)
+        return carry
+
+    lax.fori_loop(0, ROWS, fold, 0)
     copies = near_copies(part_ref, box_ref, near_sem.at[2], near_sem.at[3])
     for copy in copies:
         copy.start()
+    clear(acc_ref)
     sums = [part_ref[ROWS + y + 1][1 : QUADS + 1] for y in range(CY)]
     for d, (ox, oy, oz) in enumerate(OFFSETS):
         copies[d].wait_recv()
@@ -624,37 +661,40 @@
     inverse_windows(inv_ref, win_ref)
     compose(win_ref, tile_ref)
 
-    second_pass(turn_ref, tile_ref, ahead_ref, late_ref, zp_ref, acc_ref, stage_ref)
+    second_pass(feat_ref, tile_ref, late_ref, zp_ref, acc_ref, stage_ref)
     answer_points(stage_ref, res_ref, metas_ref, reply_ref)
     exchange_start(reply_ref, ans_ref, bsend, brecv)
     ans_ref[me] = reply_ref[me]
     uncompose(acc_ref, wide_ref, 4)
 
-    def fold_pull(xy, carry):
-        quads = fold_quads(wide_ref, xy, lane8)
-        for m in range(3):
-            pull_ref[xy, m] = jnp.where(row8 < 4, quads[2 * m], quads[2 * m + 1])
-        return carry
-
-    lax.fori_loop(0, COLUMNS, fold_pull, 0)
-    copies = near_copies(pull_ref, pulls_ref, near_sem.at[6], near_sem.at[7])
+    def fold_pull(y, carry):
+        for x in range(3):
+            quads = fold_quads(wide_ref, x * ROWS + y, lane8)
+            for m, (low, high) in enumerate(((1, 2), (3, 4), (0, 5))):
+                pull_ref[m, x * ROWS + y] = jnp.where(row8 < 4, quads[low], quads[high])
+        return carry
+
+    lax.fori_loop(0, ROWS, fold_pull, 0)
+    copies = pull_copies(pull_ref, pulls_ref, near_sem.at[6], near_sem.at[7])
     for copy in copies:
         copy.start()
-    sums = [[pull_ref[ROWS + y + 1, m] for m in range(3)] for y in range(CY)]
+    sums = [[pull_ref[m, ROWS + y + 1] for m in range(2)] for y in range(CY)]
     for d, (ox, oy, oz) in enumerate(OFFSETS):
         copies[d].wait_recv()
         for k in range(CY if oy == 0 else 1):
             y = owner_row(oy, k)
             if oz == 0:
-                for m in range(3):
-                    sums[y][m] = sums[y][m] + pulls_ref[d, k, m]
+                for m in range(2):
+                    sums[y][m] = sums[y][m] + pulls_ref[d, m, k]
             elif oz > 0:
-                sums[y][0] = sums[y][0] + jnp.where(row8 >= 4, pulls_ref[d, k, 2], 0.0)
+                outer = pltpu.roll(pulls_ref[d, 0, k], 4, 0)
+                sums[y][0] = sums[y][0] + jnp.where(row8 < 4, outer, 0.0)
             else:
-                sums[y][2] = sums[y][2] + jnp.where(row8 < 4, pulls_ref[d, k, 0], 0.0)
+                outer = pltpu.roll(pulls_ref[d, 0, k], 4, 0)
+                sums[y][1] = sums[y][1] + jnp.where(row8 >= 4, outer, 0.0)
     for y in range(CY):
         for q in range(QUADS):
-            m, half = divmod(q + 1, 2)
+            m, half = divmod(q, 2)
             tile = sums[y][m][4 * half : 4 * half + 4]
             loss = loss_ref[y][q : q + 1]
             opacity = loss_ref[y][QUADS + q : QUADS + q + 1]
@@ -662,30 +702,37 @@
             dense = loss - WIDTH * (tile / jnp.where(valid, opacity, 1.0))
             tile = jnp.where(iota((4, LANES), 0) < 3, tile * (-BACK), dense)
             tile = jnp.where(valid, tile, 0.0)
-            for r in range(4):
-                grad_ref[0, y, 4 * q + r] = tile[:, SLOTS * r : SLOTS * r + SLOTS]
+            parts = [tile[:, SLOTS * r : SLOTS * r + SLOTS] for r in range(4)]
+            for r in (0, 2):
+                both = jnp.concatenate(parts[r : r + 2], axis=0)
+                grad_ref[pl.ds(4 * (y * CZ + 4 * q + r), 8), :] = both
     for copy in copies:
         copy.wait_send()
     exchange_wait(reply_ref, ans_ref, bsend, brecv)
 
-    def place(b, carry):
-        cell = cell_ref[b]
-        brick = ((cell >> 10 & 7) * SY + (cell >> 8 & 3)) * SZ + (cell >> 4 & 3)
-        tile = ans_ref[brick]
-        tile = jnp.where(homes_ref[0, brick] == b, tile, pltpu.roll(tile, 4, 0))
-        point_ref[b] = tile[0:4]
-        return carry
-
-    lax.fori_loop(0, BLOCKS, place, 0)
+    def place(i, carry):
+        for u in range(4):
+            tiles = []
+            for k in range(2):
+                b = i * 8 + u * 2 + k
+                cell = cell_ref[b]
+                brick = ((cell >> 10 & 7) * SY + (cell >> 8 & 3)) * SZ + (cell >> 4 & 3)
+                tile = ans_ref[brick]
+                half = (homes_ref[0, brick] != b).astype(I32)
+                tiles.append(jnp.where(half == k, tile, pltpu.roll(tile, 4, 0)))
+            point_ref[pl.ds(pl.multiple_of(i * 32 + u * 8, 8), 8), :] = jnp.where(row8 < 4, tiles[0], tiles[1])
+        return carry
+
+    lax.fori_loop(0, BLOCKS // 8, place, 0)
 
 
 def on_device(point_xyz, point_weight, block_cell, block_count, gauss_mean, gauss_opacity, gauss_count):
     dma = pltpu.SemaphoreType.DMA
-    return pl.pallas_call(
+    point_out, gauss_grad = pl.pallas_call(
         kernel,
         out_shape=(
-            jax.ShapeDtypeStruct((BLOCKS, 4, LANES), F32),
-            jax.ShapeDtypeStruct((1, CY, CZ, 4, SLOTS), F32),
+            jax.ShapeDtypeStruct((BLOCKS * 4, LANES), F32),
+            jax.ShapeDtypeStruct((CELLS * 4, SLOTS), F32),
         ),
         in_specs=[SMEM, SMEM, SMEM, VMEM, VMEM, VMEM, VMEM],
         out_specs=(VMEM, VMEM),
@@ -701,10 +748,10 @@
             pltpu.VMEM((CELLS, TILES, 8, LANES), F32),
             pltpu.VMEM((CELLS + 8, LANES), I32),
             pltpu.SMEM((CELLS + 8, LANES), I32),
-            pltpu.VMEM((CELLS, LANES, 8), F32),
-            pltpu.VMEM((4 * GROUPS, 8, LANES), F32),
-            pltpu.VMEM((4 * GROUPS, 8, LANES), F32),
-            pltpu.VMEM((ITEMS * GROUPS, 8, LANES), F32),
+            pltpu.VMEM((CELLS + 1, 8, LANES), F32),
+            pltpu.VMEM((4, (CELLS + 1) * 16, 8, LANES), F32),
+            pltpu.VMEM((4 * SECOND_GROUPS, 8, LANES), F32),
+            pltpu.VMEM((CELLS * 16, 8, LANES), F32),
             pltpu.VMEM((CELLS, 4 * TILES, 8, LANES), F32),
             pltpu.VMEM((CZ, COLUMNS, 8, LANES), F32),
             pltpu.VMEM((COLUMNS, 8, LANES), F32),
@@ -715,8 +762,8 @@
             pltpu.VMEM((CELLS, 8, LANES), F32),
             pltpu.VMEM((BRICKS, 8, LANES), F32),
             pltpu.VMEM((BRICKS, 8, LANES), F32),
-            pltpu.VMEM((COLUMNS, 3, 8, LANES), F32),
-            pltpu.VMEM((26, CY, 3, 8, LANES), F32),
+            pltpu.VMEM((3, COLUMNS, 8, LANES), F32),
+            pltpu.VMEM((26, 2, CY, 8, LANES), F32),
             dma((2,)),
             dma((BRICKS,)),
             dma((BRICKS,)),
@@ -728,7 +775,16 @@
             collective_id=0, has_side_effects=True, vmem_limit_bytes=56 * 1024 * 1024
         ),
         name="chamfer",
-    )(block_cell, block_count, gauss_count, point_xyz, point_weight, gauss_mean, gauss_opacity)
+    )(
+        block_cell,
+        block_count,
+        gauss_count,
+        point_xyz.transpose(1, 0, 2),
+        point_weight,
+        gauss_mean.transpose(0, 1, 3, 2, 4),
+        gauss_opacity,
+    )
+    return point_out.reshape(BLOCKS, 4, LANES), gauss_grad.reshape(1, CY, CZ, 4, SLOTS)
 
 
 def solution(mesh):

time: 189 us -> 120 us (0.63)
  Pallas kernels: 184 us -> 117 us
  local copies, waits for them, and re-layouts: 4.54 us -> 2.23 us
    pallas_call x1, Pallas kernels: 184 us -> 117 us  [on_device(): pl.pallas_call(kernel, out_shape=(jax.ShapeDtypeStruct((BLOCKS * 4, LANES...]
    unnamed x8 -> x4, local copies, waits for them, and re-layouts: 4.54 us -> 2.23 us
where the time goes in v3:
time: 120 us
  Pallas kernels  117 us (98%)
  local copies, waits for them, and re-layouts  2.23 us (2%)
    pallas_call x1, Pallas kernels, on_device(): pl.pallas_call(kernel, out_shape=(jax.ShapeDtypeStruct((BLOCKS * 4, LANES...  117 us

profile of v3, /device:TPU:1, one launch (start us, length us, event | category | flops | bytes accessed | tf_op | source)
XLA Modules:
  0.0 120.1 jit_solution(2419772920033463548)
XLA Ops:
  0.6 117.2 %chamfer.1 = (f32[192,128]{1,0:T(8,128)}, f32[256,32]{1,0:T(8,128)}) custom-call(s32[48]{0:T(128)} %cell_ref.1, s32[48]{0:T(128)} %count_ref.1, s32[1,4,16]{2,1,0:T(4,128)} %gcount_ref.1, f32[3,48,128]{2,1,0:T(8,128)} %bitcast.7, f32[48,128]{1,0:T(8,128)} %weight_ref.1, f32[1,4,3,16,32]{4,3,2,1,0:T(8,128)} %bitcast.5, f32[1,4,16,32]{3,2,1,0:T(8,128)} %opacity_ref.1), custom_call_target="tpu_custom_call" | custom-call | tf_op jit(solution)/shard_map/chamfer/pallas_call | solution.py:731
  117.8 0.0 copy-start
  117.8 1.6 %copy.11 = f32[48,4,128]{2,1,0:T(4,128)} copy(f32[48,4,128]{2,1,0:T(4,128)} %bitcast.6) | data formatting | bytes 196608
  119.4 0.0 copy-done
  119.4 0.7 copy.12
Async XLA Ops:
  117.8 1.6 %copy-start = (f32[256,32]{1,0:T(8,128)S(1)}, f32[256,32]{1,0:T(8,128)}, u32[]{:S(2)}) copy-start(f32[256,32]{1,0:T(8,128)} %get-tuple-element.5) | copy-start | bytes 98308

commit v4 on v3

--- a/solution.py
+++ b/solution.py
@@ -17,8 +17,10 @@
 SLOTS = 32
 LANES = 128
 QUADS = CZ // 4
-FIRST_GROUPS = 8
-SECOND_GROUPS = 4
+GROUPS = 16
+HALF = 8
+PART = 8
+FEATURE = (CELLS + 1) * GROUPS
 TILES = 7
 ROWS = CY + 2
 COLUMNS = 3 * ROWS
@@ -348,7 +350,7 @@
     lax.fori_loop(0, CZ, one, 0)
 
 
-def uncompose(acc_ref, wide_ref, count):
+def uncompose(tile_of, wide_ref, count):
     row8 = iota((8, LANES), 0)
     lane8 = iota((8, LANES), 1)
 
@@ -358,7 +360,7 @@
             tiles = []
             for j in range(TILES):
                 at = y * CZ + z
-                rows = [jnp.sum(acc_ref[at, j * count + k], axis=0, keepdims=True) for k in range(count)]
+                rows = [jnp.sum(tile_of(at, j, k), axis=0, keepdims=True) for k in range(count)]
                 tile = spread(rows[0])
                 for k in range(1, count):
                     tile = jnp.where((row8 & 3) == k, rows[k], tile)
@@ -376,10 +378,10 @@
     lax.fori_loop(0, CZ, one, 0)
 
 
-def clear(acc_ref):
+def clear(ref):
     def one(c, carry):
-        for j in range(4 * TILES):
-            acc_ref[c, j] = jnp.zeros((8, LANES), F32)
+        for j in range(ref.shape[1]):
+            ref[c, j] = jnp.zeros((8, LANES), F32)
         return carry
 
     lax.fori_loop(0, CELLS, one, 0)
@@ -447,119 +449,134 @@
             tile = jnp.where((safe & 1) == 1, pltpu.roll(tile, 4, 0), tile)
             tile = jnp.where(slot >= 0, tile, 0.0)
             shift = origin + jnp.where(row8 == 2, (c % CZ).astype(F32), 0.0)
-            weight = jnp.where(tile > 0.0, jnp.log2(jnp.maximum(tile, 1e-30)), GONE)
-            pts_ref[c] = jnp.where(row8 == 3, weight, (tile - shift) * scale)
+            pts_ref[c] = (tile - shift) * scale
         return carry
 
     lax.fori_loop(0, CELLS // 8, prepare, 0)
     pts_ref[CELLS] = jnp.zeros((8, LANES), F32)
 
 
-def rows_of(i, groups):
-    chunks = LANES // (8 * groups)
-    return i // chunks, i % chunks * (8 * groups)
-
-
-def turn(pts_ref, feat_ref, c, f):
+def turn(pts_ref, feat_ref, c, f, at):
     row = jnp.broadcast_to(pts_ref[c, pl.ds(f, 1), :], (LANES, LANES))
-    feat_ref[f, pl.ds(c * 16, 16)] = jnp.transpose(row).reshape(16, 8, LANES)
-
-
-def first_pass(pts_ref, feat_ref, tile_ref, late_ref, zp_ref, acc_ref):
-    groups = FIRST_GROUPS
-    items = CELLS * LANES // (8 * groups)
+    feat_ref[pl.ds(at, GROUPS)] = jnp.transpose(row).reshape(GROUPS, 8, LANES)
+
+
+def first_pass(pts_ref, feat_ref, tile_ref, late_ref, term_a_ref, term_b_ref, ip_ref, acc_ref, dens_ref, pull_ref):
+    weights = 3 * FEATURE
     for f in range(4):
-        turn(pts_ref, feat_ref, 0, f)
-    for g in range(groups):
-        late_ref[g] = jnp.zeros((8, LANES), F32)
-
-    def settle(i):
-        for g in range(groups):
-            total = jnp.sum(late_ref[g], axis=1, keepdims=True)
-            zp_ref[i * groups + g] = jnp.broadcast_to(total, (8, LANES))
-
-    def sweep(i, carry):
-        feats = [[feat_ref[f, i * groups + g] for f in range(4)] for g in range(groups)]
-        settle((i + items - 1) % items)
-        for f in range(2):
-            turn(pts_ref, feat_ref, i // 2 + 1, i % 2 * 2 + f)
-        c, first = rows_of(i, groups)
-        sums = [None] * groups
+        turn(pts_ref, feat_ref, 0, f, f * FEATURE)
+    for g in range(PART):
+        late_ref[PART + g] = jnp.zeros((8, LANES), F32)
+    for k in range(TILES * PART):
+        term_b_ref[k] = jnp.zeros((8, LANES), F32)
+
+    def weight_of(c, g):
+        return feat_ref[weights + c % 2 * GROUPS + g]
+
+    def settle(c, part, term_ref, weight=None):
+        weight = [weight_of(c, part * PART + g) for g in range(PART)] if weight is None else weight
+        inverse = []
+        for g in range(PART):
+            at = part * PART + g
+            total = jnp.sum(late_ref[at], axis=1, keepdims=True)
+            inverse.append(1.0 / (FLOOR + jnp.broadcast_to(total, (8, LANES))))
+            ip_ref[c * GROUPS + at] = jnp.where(weight[g] > 0.0, inverse[g], 1.0)
+        for j in range(TILES):
+            dense = dens_ref[c, j]
+            for g in range(PART):
+                dense = dense + term_ref[PART * j + g] * inverse[g]
+            dens_ref[c, j] = dense
+
+    def features(c, part):
+        base = c * GROUPS + part * PART
+        feats = [[feat_ref[f * FEATURE + base + g] for f in range(3)] for g in range(PART)]
+        return feats, [weight_of(c, part * PART + g) for g in range(PART)]
+
+    def main(c, part, term_ref, feats, weight):
+        base = c * GROUPS + part * PART
+        sums = [None] * PART
         for j in range(TILES):
             mx, my, mz, la = [spread(tile_ref[c, j, f : f + 1, :]) for f in range(4)]
             far = None
-            for g in range(groups):
-                px, py, pz, lw = feats[g]
+            for g in range(PART):
+                px, py, pz = feats[g]
                 ex, ey, ez = px - mx, py - my, pz - mz
                 fall = jnp.exp2(LIFT - ex * ex - ey * ey - ez * ez)
-                term = jnp.exp2(fall + (la + lw))
-                sums[g] = term if sums[g] is None else sums[g] + term
+                near = jnp.exp2(fall + la)
+                term = near * weight[g]
+                sums[g] = near if sums[g] is None else sums[g] + near
                 far = term if far is None else far + term
-            acc_ref[c, j] = acc_ref[c, j] + far
-        for g in range(groups):
-            late_ref[g] = sums[g]
-        return carry
-
-    lax.fori_loop(0, items, sweep, 0)
-    settle(items - 1)
-
-
-def second_pass(feat_ref, tile_ref, late_ref, zp_ref, acc_ref, stage_ref):
-    groups = SECOND_GROUPS
-    items = CELLS * LANES // (8 * groups)
-    for g in range(4 * groups):
+                term_ref[PART * j + g] = term
+                pull_ref[base + g, j] = term * fall
+            acc_ref[c, 3 * j] = acc_ref[c, 3 * j] + far
+        for g in range(PART):
+            late_ref[part * PART + g] = sums[g]
+
+    def sweep(c, carry):
+        loaded = [features(c, part) for part in range(2)]
+        settle((c + CELLS - 1) % CELLS, 1, term_b_ref)
+        ahead = (c + 1) * GROUPS
+        for f in range(3):
+            turn(pts_ref, feat_ref, c + 1, f, f * FEATURE + ahead)
+        turn(pts_ref, feat_ref, c + 1, 3, weights + (c + 1) % 2 * GROUPS)
+        main(c, 0, term_a_ref, *loaded[0])
+        settle(c, 0, term_a_ref, loaded[0][1])
+        main(c, 1, term_b_ref, *loaded[1])
+        return carry
+
+    lax.fori_loop(0, CELLS, sweep, 0)
+    settle(CELLS - 1, 1, term_b_ref)
+
+
+def second_pass(feat_ref, tile_ref, late_ref, ip_ref, acc_ref, pull_ref):
+    halves = CELLS * GROUPS // HALF
+    for g in range(4 * HALF):
         late_ref[g] = jnp.ones((8, LANES), F32)
     lane = iota((8, LANES), 1) & 3
 
-    def settle(i):
-        c, first = rows_of(i, groups)
-        for g in range(groups):
-            out = (WIDTH * jnp.log(late_ref[4 * g + 3]))
+    def settle(h):
+        for g in range(HALF):
+            out = WIDTH * jnp.log(late_ref[4 * g + 3])
             for k in range(3):
                 total = jnp.sum(late_ref[4 * g + k], axis=1, keepdims=True) * BACK
                 out = jnp.where(lane == k + 1, total, out)
-            stage_ref[c, pl.ds(pl.multiple_of(first + 8 * g, 8), 8), :] = out[:, 0:8]
-
-    def sweep(i, carry):
-        feats = [[feat_ref[f, i * groups + g] for f in range(4)] for g in range(groups)]
-        settle((i + items - 1) % items)
-        c, first = rows_of(i, groups)
-        inverse = []
-        for g in range(groups):
-            lw = feats[g][3]
-            total = FLOOR + zp_ref[i * groups + g] * jnp.exp2(-jnp.maximum(lw, -64.0))
-            inverse.append(jnp.where(lw > 0.5 * GONE, 1.0 / total, 1.0))
-        sums = [[None] * 3 for g in range(groups)]
+            ip_ref[h * HALF + g] = out
+
+    def sweep(h, carry):
+        c = h // 2
+        base = h * HALF
+        feats = [[feat_ref[f * FEATURE + base + g] for f in range(3)] for g in range(HALF)]
+        inverse = [ip_ref[base + g] for g in range(HALF)]
+        settle((h + halves) % (halves + 1))
+        sums = [[None] * 3 for g in range(HALF)]
         for j in range(TILES):
-            mx, my, mz, la, ig = [spread(tile_ref[c, j, f : f + 1, :]) for f in range(5)]
-            far = [None] * 4
-            for g in range(groups):
-                px, py, pz, lw = feats[g]
-                ex, ey, ez = px - mx, py - my, pz - mz
-                fall = jnp.exp2(LIFT - ex * ex - ey * ey - ez * ez)
-                term = jnp.exp2(fall + (la + lw))
-                pull = (term * fall) * (inverse[g] + ig)
-                parts = [pull * ex, pull * ey, pull * ez, term * inverse[g]]
+            mx, my, mz, ig = [spread(tile_ref[c, j, f : f + 1, :]) for f in (0, 1, 2, 4)]
+            far = [None] * 3
+            for g in range(HALF):
+                px, py, pz = feats[g]
+                pull = pull_ref[base + g, j] * (inverse[g] + ig)
+                parts = [pull * (px - mx), pull * (py - my), pull * (pz - mz)]
                 sums[g] = [p if s is None else s + p for s, p in zip(sums[g], parts)]
                 far = [p if s is None else s + p for s, p in zip(far, parts)]
-            for k in range(4):
-                acc_ref[c, 4 * j + k] = acc_ref[c, 4 * j + k] + far[k]
-        for g in range(groups):
+            for k in range(3):
+                acc_ref[c, 3 * j + k] = acc_ref[c, 3 * j + k] + far[k]
+        for g in range(HALF):
             for k in range(3):
                 late_ref[4 * g + k] = sums[g][k]
             late_ref[4 * g + 3] = inverse[g]
         return carry
 
-    lax.fori_loop(0, items, sweep, 0)
-    settle(items - 1)
-
-
-def answer_points(stage_ref, res_ref, metas_ref, reply_ref):
+    lax.fori_loop(0, halves, sweep, 0)
+    settle(halves - 1)
+
+
+def answer_points(ip_ref, res_ref, metas_ref, reply_ref):
     row8 = iota((8, LANES), 0)
 
     def turn(i, carry):
         for u in range(8):
-            res_ref[i * 8 + u] = jnp.transpose(stage_ref[i * 8 + u])
+            tall = ip_ref[pl.ds((i * 8 + u) * GROUPS, GROUPS)].reshape(LANES, LANES)
+            res_ref[i * 8 + u] = jnp.transpose(tall)[0:8]
         return carry
 
     lax.fori_loop(0, CELLS // 8, turn, 0)
@@ -591,8 +608,8 @@
 def kernel(cell_ref, count_ref, gcount_ref, xyz_ref, weight_ref, mean_ref, opacity_ref,
            point_ref, grad_ref,
            pay_ref, out_ref, in_ref, home_ref, homes_ref, gauss_ref, halo_ref, win_ref, tile_ref,
-           meta_ref, metas_ref, pts_ref, feat_ref, late_ref, zp_ref, acc_ref, wide_ref, part_ref,
-           box_ref, inv_ref, loss_ref, stage_ref, res_ref, reply_ref, ans_ref, pull_ref, pulls_ref,
+           meta_ref, metas_ref, pts_ref, feat_ref, late_ref, term_a_ref, term_b_ref, ip_ref, keep_ref, acc_ref, dens_ref, wide_ref, part_ref,
+           box_ref, inv_ref, loss_ref, res_ref, ans_ref, pull_ref, pulls_ref,
            local_sem, asend, arecv, bsend, brecv, near_sem):
     gx, gy, gz = here()
     me = (gx * SY + gy) * SZ + gz
@@ -618,12 +635,13 @@
     feature_windows(halo_ref, win_ref, origin, scale)
     compose(win_ref, tile_ref)
     clear(acc_ref)
+    clear(dens_ref)
     exchange_wait(out_ref, in_ref, asend, arecv)
     decode(in_ref, meta_ref, metas_ref, local_sem.at[1])
     take_points(in_ref, metas_ref, pts_ref, origin, scale)
 
-    first_pass(pts_ref, feat_ref, tile_ref, late_ref, zp_ref, acc_ref)
-    uncompose(acc_ref, wide_ref, 1)
+    first_pass(pts_ref, feat_ref, tile_ref, late_ref, term_a_ref, term_b_ref, ip_ref, acc_ref, dens_ref, keep_ref)
+    uncompose(lambda c, j, k: acc_ref[c, 3 * j], wide_ref, 1)
 
     def fold(y, carry):
         for x in range(3):
@@ -661,11 +679,12 @@
     inverse_windows(inv_ref, win_ref)
     compose(win_ref, tile_ref)
 
-    second_pass(feat_ref, tile_ref, late_ref, zp_ref, acc_ref, stage_ref)
-    answer_points(stage_ref, res_ref, metas_ref, reply_ref)
+    second_pass(feat_ref, tile_ref, late_ref, ip_ref, acc_ref, keep_ref)
+    reply_ref = out_ref
+    answer_points(ip_ref, res_ref, metas_ref, reply_ref)
     exchange_start(reply_ref, ans_ref, bsend, brecv)
     ans_ref[me] = reply_ref[me]
-    uncompose(acc_ref, wide_ref, 4)
+    uncompose(lambda c, j, k: acc_ref[c, 3 * j + k] if k < 3 else dens_ref[c, j], wide_ref, 4)
 
     def fold_pull(y, carry):
         for x in range(3):
@@ -749,18 +768,20 @@
             pltpu.VMEM((CELLS + 8, LANES), I32),
             pltpu.SMEM((CELLS + 8, LANES), I32),
             pltpu.VMEM((CELLS + 1, 8, LANES), F32),
-            pltpu.VMEM((4, (CELLS + 1) * 16, 8, LANES), F32),
-            pltpu.VMEM((4 * SECOND_GROUPS, 8, LANES), F32),
-            pltpu.VMEM((CELLS * 16, 8, LANES), F32),
-            pltpu.VMEM((CELLS, 4 * TILES, 8, LANES), F32),
+            pltpu.VMEM((3 * FEATURE + 2 * GROUPS, 8, LANES), F32),
+            pltpu.VMEM((4 * HALF, 8, LANES), F32),
+            pltpu.VMEM((TILES * PART, 8, LANES), F32),
+            pltpu.VMEM((TILES * PART, 8, LANES), F32),
+            pltpu.VMEM((CELLS * GROUPS + HALF, 8, LANES), F32),
+            pltpu.VMEM((CELLS * GROUPS, TILES, 8, LANES), F32),
+            pltpu.VMEM((CELLS, 3 * TILES, 8, LANES), F32),
+            pltpu.VMEM((CELLS, TILES, 8, LANES), F32),
             pltpu.VMEM((CZ, COLUMNS, 8, LANES), F32),
             pltpu.VMEM((COLUMNS, 8, LANES), F32),
             pltpu.VMEM((26, CY, 8, LANES), F32),
             pltpu.VMEM((3, COLUMNS, 8, LANES), F32),
             pltpu.VMEM((CY, 8, LANES), F32),
-            pltpu.VMEM((CELLS, LANES, 8), F32),
             pltpu.VMEM((CELLS, 8, LANES), F32),
-            pltpu.VMEM((BRICKS, 8, LANES), F32),
             pltpu.VMEM((BRICKS, 8, LANES), F32),
             pltpu.VMEM((3, COLUMNS, 8, LANES), F32),
             pltpu.VMEM((26, 2, CY, 8, LANES), F32),
@@ -772,7 +793,7 @@
             dma((8, 26)),
         ],
         compiler_params=pltpu.CompilerParams(
-            collective_id=0, has_side_effects=True, vmem_limit_bytes=56 * 1024 * 1024
+            collective_id=0, has_side_effects=True, vmem_limit_bytes=67043328
         ),
         name="chamfer",
     )(

time: 120 us -> 114 us (0.950)
  Pallas kernels: 117 us -> 111 us
    pallas_call x1, Pallas kernels: 117 us -> 111 us  [on_device(): pl.pallas_call(kernel, out_shape=(jax.ShapeDtypeStruct((BLOCKS * 4, LANES...]
where the time goes in v4:
time: 114 us; the launch traced here: 113 us
  Pallas kernels  111 us (97%)
  local copies, waits for them, and re-layouts  2.23 us (2%)
    pallas_call x1, Pallas kernels, on_device(): pl.pallas_call(kernel, out_shape=(jax.ShapeDtypeStruct((BLOCKS * 4, LANES...  111 us

profile of v4, /device:TPU:1, one launch (start us, length us, event | category | flops | bytes accessed | tf_op | source)
XLA Modules:
  0.0 113.4 jit_solution(1549934638984087433)
XLA Ops:
  0.6 110.5 %chamfer.1 = (f32[192,128]{1,0:T(8,128)}, f32[256,32]{1,0:T(8,128)}) custom-call(s32[48]{0:T(128)} %cell_ref.1, s32[48]{0:T(128)} %count_ref.1, s32[1,4,16]{2,1,0:T(4,128)} %gcount_ref.1, f32[3,48,128]{2,1,0:T(8,128)} %bitcast.7, f32[48,128]{1,0:T(8,128)} %weight_ref.1, f32[1,4,3,16,32]{4,3,2,1,0:T(8,128)} %bitcast.5, f32[1,4,16,32]{3,2,1,0:T(8,128)} %opacity_ref.1), custom_call_target="tpu_custom_call" | custom-call | tf_op jit(solution)/shard_map/chamfer/pallas_call | solution.py:750
  111.2 0.0 copy-start
  111.2 1.6 %copy.11 = f32[48,4,128]{2,1,0:T(4,128)} copy(f32[48,4,128]{2,1,0:T(4,128)} %bitcast.6) | data formatting | bytes 196608
  112.8 0.0 copy-done
  112.8 0.7 copy.12
Async XLA Ops:
  111.2 1.6 %copy-start = (f32[256,32]{1,0:T(8,128)S(1)}, f32[256,32]{1,0:T(8,128)}, u32[]{:S(2)}) copy-start(f32[256,32]{1,0:T(8,128)} %get-tuple-element.5) | copy-start | bytes 98308
